TPU v7x, 256 devices: a whole 4x4x8 slice. The times are simulated.
256 devices in a mesh: gx: 32 (over z_hi, y, core), gy: 8 (over x, z_lo).
Axes of the slice: x: 4, y: 4, z: 8 (z_hi: 4, z_lo: 2; z = z_hi * 2 + z_lo), core: 2. Of those that a mesh axis runs over, the one named last changes fastest.
Arguments:
- innovation: float32 [2, 1536, 1536], P(None, 'gx', 'gy'), may hold values from -6 to 6
- obs_weight: float32 [2, 1536, 1536], P(None, 'gx', 'gy'), may hold values from 0.2 to 2
- static_scale: float32 [2, 1536, 1536], P(None, 'gx', 'gy'), may hold values from 0.3 to 1.5
- members: bfloat16 [36, 2, 512, 512], P(None, None, ('gx', 'gy')), may hold values from -1 to 1
- diffusivity: bfloat16 [2, 512, 512], P(None, ('gx', 'gy')), may hold values from 0.049804688 to 0.23925781
Outputs:
- increment: float32 [2, 1536, 1536], P(None, 'gx', 'gy')
- static_control: float32 [2, 1536, 1536], P(None, 'gx', 'gy')
All inputs are finite; a program needn't handle non-finite values.
Results may differ from a plain program's by a relative error of at most 0.0004.
Values may be sent and summed in bfloat16 or wider, within the bound.
A program may use at most 64 MiB of HBM per device.

v0:
```python
import functools

import jax
import jax.numpy as jnp
from jax import lax
from jax.sharding import Mesh
from jax.sharding import PartitionSpec as P

NPASS = 4
ITERS = 3
GX_GY = ("gx_0", "gx_1", "gx_2", "gy_0", "gy_1")
GY = ("gy_0", "gy_1")
GX = ("gx_0", "gx_1", "gx_2")


THIRD = 1.0 / 3.0
TWO_THIRDS = 2.0 / 3.0


def extended(x, sides, width):
    edges = {}
    for axis, dim in sides:
        size, length = (lax.axis_size(axis), x.shape[dim])
        up = [(i, (i + 1) % size) for i in range(size - 1)]
        last = lax.slice_in_dim(x, length - width, length, axis=dim)
        leading = lax.slice_in_dim(x, 0, width, axis=dim)
        edges[dim] = (
            lax.ppermute(last, axis, up),
            lax.ppermute(leading, axis, [(b, a) for a, b in up]),
        )
    done = []
    for _, dim in sides:
        low, high = edges[dim]
        around = [(width, width) if d in done else (0, 0) for d in range(x.ndim)]
        x = jnp.concatenate([jnp.pad(low, around), x, jnp.pad(high, around)], axis=dim)
        done.append(dim)
    return x


def with_halo(block, sides, width):
    for axis, dim in sides:
        count = lax.axis_size(axis)
        forward = [(i, i + 1) for i in range(count - 1)]
        backward = [(target, source) for source, target in forward]
        low = lax.ppermute(
            lax.slice_in_dim(block, block.shape[dim] - width, None, axis=dim), axis, forward
        )
        high = lax.ppermute(lax.slice_in_dim(block, 0, width, axis=dim), axis, backward)
        block = jnp.concatenate([low, block, high], axis=dim)
    return block


def over_axes(x, axes):
    return functools.reduce(lax.psum, axes, x)


def laplace_padded(padded):
    center = padded[..., 1:-1, 1:-1]
    return (
        padded[..., 2:, 1:-1]
        + padded[..., :-2, 1:-1]
        + padded[..., 1:-1, 2:]
        + padded[..., 1:-1, :-2]
        - 4.0 * center
    )


def prolong_axis(padded, along):
    length = padded.shape[along] - 2
    lowers = lax.slice_in_dim(padded, 0, length, axis=along)
    middle = lax.slice_in_dim(padded, 1, length + 1, axis=along)
    uppers = lax.slice_in_dim(padded, 2, length + 2, axis=along)
    stacked = jnp.stack(
        [lowers * THIRD + middle * TWO_THIRDS, middle, middle * TWO_THIRDS + uppers * THIRD],
        axis=along,
    )
    target = list(middle.shape)
    target[along] = 3 * length
    return stacked.reshape(target)


def restrict_axis(padded, along):
    length = padded.shape[along] - 2
    position = padded.ndim + along
    count = length // 3

    def reshaped(start):
        portion = lax.slice_in_dim(padded, start, start + length, axis=along)
        target = list(portion.shape[:position]) + [count, 3] + list(portion.shape[position + 1 :])
        return portion.reshape(target)

    left_side = lax.index_in_dim(reshaped(0), 0, position + 1, keepdims=False)
    centred = reshaped(1)
    right_side = lax.index_in_dim(reshaped(2), 2, position + 1, keepdims=False)
    first = lax.index_in_dim(centred, 0, position + 1, keepdims=False)
    second = lax.index_in_dim(centred, 1, position + 1, keepdims=False)
    third = lax.index_in_dim(centred, 2, position + 1, keepdims=False)
    return left_side * THIRD + first * TWO_THIRDS + second + third * TWO_THIRDS + right_side * THIRD


def widen(values):
    padded = extended(values.astype(jnp.bfloat16), ((GX_GY, 2),), 1).astype(values.dtype)
    return jnp.pad(padded, ((0, 0), (0, 0), (0, 0), (1, 1)))


def forward(static_part, amplitude, members, rates, static_scale):
    for repeat in range(NPASS):
        amplitude = amplitude + rates * laplace_padded(widen(amplitude))
    coarse = jnp.sum(members.astype(jnp.float32) * amplitude, axis=0)
    coarse = lax.all_to_all(coarse, GY, split_axis=2, concat_axis=1, tiled=True)
    padded = with_halo(coarse, ((GX, 1), (GY, 2)), 1)
    return static_scale * static_part + prolong_axis(prolong_axis(padded, -1), -2)


def adjoint(weighted, members, rates, static_scale):
    padded = with_halo(weighted, ((GX, 1), (GY, 2)), 1)
    coarse = restrict_axis(restrict_axis(padded, -2), -1)
    coarse = lax.all_to_all(coarse, GY, split_axis=1, concat_axis=2, tiled=True)
    amplitude = members.astype(jnp.float32) * coarse[None]
    for repeat in range(NPASS):
        amplitude = amplitude + laplace_padded(widen(rates * amplitude))
    return (static_scale * weighted, amplitude)


def inner(left, right):
    return jnp.sum(left[0] * right[0]) + jnp.sum(left[1] * right[1])


def advance(first, scale, second):
    return (first[0] + scale * second[0], first[1] + scale * second[1])


def paired(residual, curved):
    return (over_axes(inner(residual, residual), GX_GY), over_axes(inner(residual, curved), GX_GY))


def per_device(innovation, obs_weight, static_scale, members, diffusivity):
    rates = diffusivity.astype(jnp.float32)

    def hessian(control):
        pushed = forward(control[0], control[1], members, rates, static_scale)
        back = adjoint(obs_weight * pushed, members, rates, static_scale)
        return ((control[0] + back[0], control[1] + back[1]), pushed)

    right_hand = adjoint(obs_weight * innovation, members, rates, static_scale)
    control = (jnp.zeros_like(right_hand[0]), jnp.zeros_like(right_hand[1]))
    increment = jnp.zeros_like(innovation)
    residual = right_hand
    curved, pushed = hessian(residual)
    norm_now, product = paired(residual, curved)
    step_size = norm_now / product
    direction = residual
    along = curved
    carried = pushed
    for repeat in range(ITERS):
        control = advance(control, step_size, direction)
        increment = increment + step_size * carried
        residual = advance(residual, -step_size, along)
        if repeat + 1 < ITERS:
            curved, pushed = hessian(residual)
            norm_next, product = paired(residual, curved)
            weight_ratio = norm_next / norm_now
            step_size = norm_next / (product - weight_ratio * norm_next / step_size)
            direction = advance(residual, weight_ratio, direction)
            along = advance(curved, weight_ratio, along)
            carried = pushed + weight_ratio * carried
            norm_now = norm_next
    return (increment, control[0])


def solution(mesh):
    finer = Mesh(mesh.devices.reshape(4, 4, 2, 4, 2), ("gx_0", "gx_1", "gx_2", "gy_0", "gy_1"))
    in_specs = (
        P(None, GX, GY),
        P(None, GX, GY),
        P(None, GX, GY),
        P(None, None, GX_GY, None),
        P(None, GX_GY, None),
    )
    out_specs = (P(None, GX, GY), P(None, GX, GY))
    return jax.shard_map(
        per_device, mesh=finer, in_specs=in_specs, out_specs=out_specs, check_vma=False
    )
```

profile of v0, /device:TPU:1, one launch (start us, length us, event | category | flops | bytes accessed | tf_op | source)
XLA Modules:
  0.0 813.6 jit_solution(12217400788598385253)
XLA Ops:
  137.6 14.3 %all_to_all.114 = f32[8,1,256]{2,1,0:T(1,128)S(1)} all-to-all(f32[8,1,256]{2,1,0:T(1,128)S(1)} %reshape.231), channel_id=1, replica_groups=mesh['gx_0'=4,'gx_1'=4,'gx_2'=2,'gy_0'=4,'gy_1'=2] {'gy_0','gy_1'}, dimensions={0} | all-to-all | bytes 16384 | tf_op jit(solution)/shard_map/all_to_all | solution.py:110
  191.4 8.5 %all_to_all.115 = f32[8,1,256]{2,1,0:T(1,128)S(1)} all-to-all(f32[8,1,256]{2,1,0:T(1,128)S(1)} %reshape.233), channel_id=1, replica_groups=mesh['gx_0'=4,'gx_1'=4,'gx_2'=2,'gy_0'=4,'gy_1'=2] {'gy_0','gy_1'}, dimensions={0} | all-to-all | bytes 16384 | tf_op jit(solution)/shard_map/all_to_all | solution.py:118
  253.8 38.7 %all-reduce.36 = (f32[]{:T(128)}, f32[]{:T(128)}) all-reduce(f32[]{:T(128)S(6)} %add.737, f32[]{:T(128)S(6)} %add.787), channel_id=1, replica_groups=mesh['gx_0'=4,'gx_1'=4,'gx_2'=2,'gy_0'=4,'gy_1'=2] {'gx_0'}, use_global_device_ids=true, to_apply=%region_2.3 | all-reduce | flops 2 | bytes 16 | tf_op jit(solution)/shard_map/psum | solution.py:54
  292.4 14.0 %all-reduce.33 = (f32[]{:T(128)}, f32[]{:T(128)}) all-reduce(f32[]{:T(128)} %get-tuple-element.40, f32[]{:T(128)} %get-tuple-element.41), channel_id=1, replica_groups=mesh['gx_0'=4,'gx_1'=4,'gx_2'=2,'gy_0'=4,'gy_1'=2] {'gx_1'}, use_global_device_ids=true, to_apply=%region_3.4 | all-reduce | flops 2 | bytes 16 | tf_op jit(solution)/shard_map/psum | solution.py:54
  306.4 15.8 %all-reduce.42 = (f32[]{:T(128)}, f32[]{:T(128)}) all-reduce(f32[]{:T(128)} %get-tuple-element.34, f32[]{:T(128)} %get-tuple-element.35), channel_id=1, replica_groups=mesh['gx_0'=4,'gx_1'=4,'gx_2'=2,'gy_0'=4,'gy_1'=2] {'gx_2'}, use_global_device_ids=true, to_apply=%region_4.5 | all-reduce | flops 2 | bytes 16 | tf_op jit(solution)/shard_map/psum | solution.py:54
  322.2 6.7 all-reduce.30
  329.0 8.4 %all-reduce.39 = (f32[]{:T(128)}, f32[]{:T(128)}) all-reduce(f32[]{:T(128)} %get-tuple-element.28, f32[]{:T(128)} %get-tuple-element.29), channel_id=1, replica_groups=mesh['gx_0'=4,'gx_1'=4,'gx_2'=2,'gy_0'=4,'gy_1'=2] {'gy_1'}, use_global_device_ids=true, to_apply=%region_6.7 | all-reduce | flops 2 | bytes 16 | tf_op jit(solution)/shard_map/psum | solution.py:54
  377.7 6.7 collective-permute-start.43
  388.7 15.2 %all_to_all.116 = f32[8,1,256]{2,1,0:T(1,128)S(1)} all-to-all(f32[8,1,256]{2,1,0:T(1,128)S(1)} %reshape.235), channel_id=1, replica_groups=mesh['gx_0'=4,'gx_1'=4,'gx_2'=2,'gy_0'=4,'gy_1'=2] {'gy_0','gy_1'}, dimensions={0} | all-to-all | bytes 16384 | tf_op jit(solution)/shard_map/all_to_all | solution.py:110
  441.0 8.5 %all_to_all.117 = f32[8,1,256]{2,1,0:T(1,128)S(1)} all-to-all(f32[8,1,256]{2,1,0:T(1,128)S(1)} %reshape.237), channel_id=1, replica_groups=mesh['gx_0'=4,'gx_1'=4,'gx_2'=2,'gy_0'=4,'gy_1'=2] {'gy_0','gy_1'}, dimensions={0} | all-to-all | bytes 16384 | tf_op jit(solution)/shard_map/all_to_all | solution.py:118
  476.3 6.7 collective-permute-start.57
  504.2 23.1 %all-reduce.35 = (f32[]{:T(128)}, f32[]{:T(128)}) all-reduce(f32[]{:T(128)S(6)} %add.790, f32[]{:T(128)S(6)} %add.840), channel_id=1, replica_groups=mesh['gx_0'=4,'gx_1'=4,'gx_2'=2,'gy_0'=4,'gy_1'=2] {'gx_0'}, use_global_device_ids=true, to_apply=%region_17.18 | all-reduce | flops 2 | bytes 16 | tf_op jit(solution)/shard_map/psum | solution.py:54
  527.3 14.3 %all-reduce.32 = (f32[]{:T(128)}, f32[]{:T(128)}) all-reduce(f32[]{:T(128)} %get-tuple-element.38, f32[]{:T(128)} %get-tuple-element.39), channel_id=1, replica_groups=mesh['gx_0'=4,'gx_1'=4,'gx_2'=2,'gy_0'=4,'gy_1'=2] {'gx_1'}, use_global_device_ids=true, to_apply=%region_18.19 | all-reduce | flops 2 | bytes 16 | tf_op jit(solution)/shard_map/psum | solution.py:54
  541.5 14.6 %all-reduce.41 = (f32[]{:T(128)}, f32[]{:T(128)}) all-reduce(f32[]{:T(128)} %get-tuple-element.32, f32[]{:T(128)} %get-tuple-element.33), channel_id=1, replica_groups=mesh['gx_0'=4,'gx_1'=4,'gx_2'=2,'gy_0'=4,'gy_1'=2] {'gx_2'}, use_global_device_ids=true, to_apply=%region_19.20 | all-reduce | flops 2 | bytes 16 | tf_op jit(solution)/shard_map/psum | solution.py:54
  556.2 6.8 all-reduce.29
  562.9 8.4 %all-reduce.38 = (f32[]{:T(128)}, f32[]{:T(128)}) all-reduce(f32[]{:T(128)} %get-tuple-element.26, f32[]{:T(128)} %get-tuple-element.27), channel_id=1, replica_groups=mesh['gx_0'=4,'gx_1'=4,'gx_2'=2,'gy_0'=4,'gy_1'=2] {'gy_1'}, use_global_device_ids=true, to_apply=%region_21.22 | all-reduce | flops 2 | bytes 16 | tf_op jit(solution)/shard_map/psum | solution.py:54
  626.2 15.2 %all_to_all.118 = f32[8,1,256]{2,1,0:T(1,128)S(1)} all-to-all(f32[8,1,256]{2,1,0:T(1,128)S(1)} %reshape.239), channel_id=1, replica_groups=mesh['gx_0'=4,'gx_1'=4,'gx_2'=2,'gy_0'=4,'gy_1'=2] {'gy_0','gy_1'}, dimensions={0} | all-to-all | bytes 16384 | tf_op jit(solution)/shard_map/all_to_all | solution.py:110
  678.5 8.5 %all_to_all.119 = f32[8,1,256]{2,1,0:T(1,128)S(1)} all-to-all(f32[8,1,256]{2,1,0:T(1,128)S(1)} %reshape.241), channel_id=1, replica_groups=mesh['gx_0'=4,'gx_1'=4,'gx_2'=2,'gy_0'=4,'gy_1'=2] {'gy_0','gy_1'}, dimensions={0} | all-to-all | bytes 16384 | tf_op jit(solution)/shard_map/all_to_all | solution.py:118
  713.7 6.7 collective-permute-start.81
  741.5 23.0 %all-reduce.34 = (f32[]{:T(128)}, f32[]{:T(128)}) all-reduce(f32[]{:T(128)S(6)} %add.847, f32[]{:T(128)S(6)} %add.897), channel_id=1, replica_groups=mesh['gx_0'=4,'gx_1'=4,'gx_2'=2,'gy_0'=4,'gy_1'=2] {'gx_0'}, use_global_device_ids=true, to_apply=%region_32.33 | all-reduce | flops 2 | bytes 16 | tf_op jit(solution)/shard_map/psum | solution.py:54
  764.5 14.2 %all-reduce.31 = (f32[]{:T(128)}, f32[]{:T(128)}) all-reduce(f32[]{:T(128)} %get-tuple-element.36, f32[]{:T(128)} %get-tuple-element.37), channel_id=1, replica_groups=mesh['gx_0'=4,'gx_1'=4,'gx_2'=2,'gy_0'=4,'gy_1'=2] {'gx_1'}, use_global_device_ids=true, to_apply=%region_33.34 | all-reduce | flops 2 | bytes 16 | tf_op jit(solution)/shard_map/psum | solution.py:54
  778.7 14.6 %all-reduce.40 = (f32[]{:T(128)}, f32[]{:T(128)}) all-reduce(f32[]{:T(128)} %get-tuple-element.30, f32[]{:T(128)} %get-tuple-element.31), channel_id=1, replica_groups=mesh['gx_0'=4,'gx_1'=4,'gx_2'=2,'gy_0'=4,'gy_1'=2] {'gx_2'}, use_global_device_ids=true, to_apply=%region_34.35 | all-reduce | flops 2 | bytes 16 | tf_op jit(solution)/shard_map/psum | solution.py:54
  793.3 6.7 all-reduce.28
  800.0 8.4 %all-reduce.37 = (f32[]{:T(128)}, f32[]{:T(128)}) all-reduce(f32[]{:T(128)} %get-tuple-element.24, f32[]{:T(128)} %get-tuple-element.25), channel_id=1, replica_groups=mesh['gx_0'=4,'gx_1'=4,'gx_2'=2,'gy_0'=4,'gy_1'=2] {'gy_1'}, use_global_device_ids=true, to_apply=%region_36.37 | all-reduce | flops 2 | bytes 16 | tf_op jit(solution)/shard_map/psum | solution.py:54
  (429 shorter events, 485.2 us)
Async XLA Ops:
  22.0 10.3 %all-to-all-start = ((f32[8,1,256]{2,1,0:T(1,128)}), f32[8,1,256]{2,1,0:T(1,128)S(1)}, u32[]{:S(2)}, u32[]{:S(2)}) async-start(f32[8,1,256]{2,1,0:T(1,128)} %reshape.229), calls=%async_computation | async-start | bytes 16384 | tf_op jit(solution)/shard_map/all_to_all | solution.py:118
  45.8 9.0 %collective-permute-start.6 = (bf16[36,2,1,512]{3,2,1,0:T(2,128)(2,1)S(1)}, bf16[36,2,1,512]{3,2,1,0:T(2,128)(2,1)S(1)}, u32[]{:S(2)}, u32[]{:S(2)}) collective-permute-start(bf16[36,2,1,512]{3,2,1,0:T(2,128)(2,1)S(1)} %get-tuple-element.183), channel_id=1, source_target_pairs={{0,1},{1,2},{2,3},{3,4},{4,5},{5,6},{6,7},{7,8},{8,9},{9,10},{10,1... | collective-permute-start | bytes 221192 | tf_op jit(solution)/shard_map/ppermute | solution.py:28
  57.5 9.3 %collective-permute-start.8 = (bf16[36,2,1,512]{3,2,1,0:T(2,128)(2,1)S(1)}, bf16[36,2,1,512]{3,2,1,0:T(2,128)(2,1)S(1)}, u32[]{:S(2)}, u32[]{:S(2)}) collective-permute-start(bf16[36,2,1,512]{3,2,1,0:T(2,128)(2,1)S(1)} %get-tuple-element.181), channel_id=1, source_target_pairs={{0,1},{1,2},{2,3},{3,4},{4,5},{5,6},{6,7},{7,8},{8,9},{9,10},{10,1... | collective-permute-start | bytes 221192 | tf_op jit(solution)/shard_map/ppermute | solution.py:28
  70.0 9.3 %collective-permute-start.10 = (bf16[36,2,1,512]{3,2,1,0:T(2,128)(2,1)S(1)}, bf16[36,2,1,512]{3,2,1,0:T(2,128)(2,1)S(1)}, u32[]{:S(2)}, u32[]{:S(2)}) collective-permute-start(bf16[36,2,1,512]{3,2,1,0:T(2,128)(2,1)S(1)} %get-tuple-element.179), channel_id=1, source_target_pairs={{0,1},{1,2},{2,3},{3,4},{4,5},{5,6},{6,7},{7,8},{8,9},{9,10},{10,1... | collective-permute-start | bytes 221192 | tf_op jit(solution)/shard_map/ppermute | solution.py:28
  72.8 9.6 %collective-permute-start.11 = (bf16[36,2,1,512]{3,2,1,0:T(2,128)(2,1)S(1)}, bf16[36,2,1,512]{3,2,1,0:T(2,128)(2,1)S(1)}, u32[]{:S(2)}, u32[]{:S(2)}) collective-permute-start(bf16[36,2,1,512]{3,2,1,0:T(2,128)(2,1)S(1)} %get-tuple-element.180), channel_id=1, source_target_pairs={{1,0},{2,1},{3,2},{4,3},{5,4},{6,5},{7,6},{8,7},{9,8},{10,9},{11,1... | collective-permute-start | bytes 221192 | tf_op jit(solution)/shard_map/ppermute | solution.py:29
  213.0 8.9 %collective-permute-start.30 = (bf16[36,2,1,512]{3,2,1,0:T(2,128)(2,1)S(1)}, bf16[36,2,1,512]{3,2,1,0:T(2,128)(2,1)S(1)}, u32[]{:S(2)}, u32[]{:S(2)}) collective-permute-start(bf16[36,2,1,512]{3,2,1,0:T(2,128)(2,1)S(1)} %get-tuple-element.167), channel_id=1, source_target_pairs={{0,1},{1,2},{2,3},{3,4},{4,5},{5,6},{6,7},{7,8},{8,9},{9,10},{10,1... | collective-permute-start | bytes 221192 | tf_op jit(solution)/shard_map/ppermute | solution.py:28
  224.7 9.3 %collective-permute-start.32 = (bf16[36,2,1,512]{3,2,1,0:T(2,128)(2,1)S(1)}, bf16[36,2,1,512]{3,2,1,0:T(2,128)(2,1)S(1)}, u32[]{:S(2)}, u32[]{:S(2)}) collective-permute-start(bf16[36,2,1,512]{3,2,1,0:T(2,128)(2,1)S(1)} %get-tuple-element.165), channel_id=1, source_target_pairs={{0,1},{1,2},{2,3},{3,4},{4,5},{5,6},{6,7},{7,8},{8,9},{9,10},{10,1... | collective-permute-start | bytes 221192 | tf_op jit(solution)/shard_map/ppermute | solution.py:28
  237.1 8.8 %collective-permute-start.34 = (bf16[36,2,1,512]{3,2,1,0:T(2,128)(2,1)S(1)}, bf16[36,2,1,512]{3,2,1,0:T(2,128)(2,1)S(1)}, u32[]{:S(2)}, u32[]{:S(2)}) collective-permute-start(bf16[36,2,1,512]{3,2,1,0:T(2,128)(2,1)S(1)} %get-tuple-element.163), channel_id=1, source_target_pairs={{0,1},{1,2},{2,3},{3,4},{4,5},{5,6},{6,7},{7,8},{8,9},{9,10},{10,1... | collective-permute-start | bytes 221192 | tf_op jit(solution)/shard_map/ppermute | solution.py:28
  339.0 9.3 %collective-permute-start.36 = (bf16[36,2,1,512]{3,2,1,0:T(2,128)(2,1)S(1)}, bf16[36,2,1,512]{3,2,1,0:T(2,128)(2,1)S(1)}, u32[]{:S(2)}, u32[]{:S(2)}) collective-permute-start(bf16[36,2,1,512]{3,2,1,0:T(2,128)(2,1)S(1)} %get-tuple-element.161), channel_id=1, source_target_pairs={{0,1},{1,2},{2,3},{3,4},{4,5},{5,6},{6,7},{7,8},{8,9},{9,10},{10,1... | collective-permute-start | bytes 221192 | tf_op jit(solution)/shard_map/ppermute | solution.py:28
  351.5 10.2 %collective-permute-start.38 = (bf16[36,2,1,512]{3,2,1,0:T(2,128)(2,1)S(1)}, bf16[36,2,1,512]{3,2,1,0:T(2,128)(2,1)S(1)}, u32[]{:S(2)}, u32[]{:S(2)}) collective-permute-start(bf16[36,2,1,512]{3,2,1,0:T(2,128)(2,1)S(1)} %get-tuple-element.159), channel_id=1, source_target_pairs={{0,1},{1,2},{2,3},{3,4},{4,5},{5,6},{6,7},{7,8},{8,9},{9,10},{10,1... | collective-permute-start | bytes 221192 | tf_op jit(solution)/shard_map/ppermute | solution.py:28
  363.6 9.3 %collective-permute-start.40 = (bf16[36,2,1,512]{3,2,1,0:T(2,128)(2,1)S(1)}, bf16[36,2,1,512]{3,2,1,0:T(2,128)(2,1)S(1)}, u32[]{:S(2)}, u32[]{:S(2)}) collective-permute-start(bf16[36,2,1,512]{3,2,1,0:T(2,128)(2,1)S(1)} %get-tuple-element.157), channel_id=1, source_target_pairs={{0,1},{1,2},{2,3},{3,4},{4,5},{5,6},{6,7},{7,8},{8,9},{9,10},{10,1... | collective-permute-start | bytes 221192 | tf_op jit(solution)/shard_map/ppermute | solution.py:28
  375.8 9.3 %collective-permute-start.42 = (bf16[36,2,1,512]{3,2,1,0:T(2,128)(2,1)S(1)}, bf16[36,2,1,512]{3,2,1,0:T(2,128)(2,1)S(1)}, u32[]{:S(2)}, u32[]{:S(2)}) collective-permute-start(bf16[36,2,1,512]{3,2,1,0:T(2,128)(2,1)S(1)} %get-tuple-element.155), channel_id=1, source_target_pairs={{0,1},{1,2},{2,3},{3,4},{4,5},{5,6},{6,7},{7,8},{8,9},{9,10},{10,1... | collective-permute-start | bytes 221192 | tf_op jit(solution)/shard_map/ppermute | solution.py:28
  462.7 8.8 %collective-permute-start.54 = (bf16[36,2,1,512]{3,2,1,0:T(2,128)(2,1)S(1)}, bf16[36,2,1,512]{3,2,1,0:T(2,128)(2,1)S(1)}, u32[]{:S(2)}, u32[]{:S(2)}) collective-permute-start(bf16[36,2,1,512]{3,2,1,0:T(2,128)(2,1)S(1)} %get-tuple-element.151), channel_id=1, source_target_pairs={{0,1},{1,2},{2,3},{3,4},{4,5},{5,6},{6,7},{7,8},{8,9},{9,10},{10,1... | collective-permute-start | bytes 221192 | tf_op jit(solution)/shard_map/ppermute | solution.py:28
  474.2 9.7 %collective-permute-start.56 = (bf16[36,2,1,512]{3,2,1,0:T(2,128)(2,1)S(1)}, bf16[36,2,1,512]{3,2,1,0:T(2,128)(2,1)S(1)}, u32[]{:S(2)}, u32[]{:S(2)}) collective-permute-start(bf16[36,2,1,512]{3,2,1,0:T(2,128)(2,1)S(1)} %get-tuple-element.149), channel_id=1, source_target_pairs={{0,1},{1,2},{2,3},{3,4},{4,5},{5,6},{6,7},{7,8},{8,9},{9,10},{10,1... | collective-permute-start | bytes 221192 | tf_op jit(solution)/shard_map/ppermute | solution.py:28
  486.7 9.3 %collective-permute-start.58 = (bf16[36,2,1,512]{3,2,1,0:T(2,128)(2,1)S(1)}, bf16[36,2,1,512]{3,2,1,0:T(2,128)(2,1)S(1)}, u32[]{:S(2)}, u32[]{:S(2)}) collective-permute-start(bf16[36,2,1,512]{3,2,1,0:T(2,128)(2,1)S(1)} %get-tuple-element.147), channel_id=1, source_target_pairs={{0,1},{1,2},{2,3},{3,4},{4,5},{5,6},{6,7},{7,8},{8,9},{9,10},{10,1... | collective-permute-start | bytes 221192 | tf_op jit(solution)/shard_map/ppermute | solution.py:28
  489.0 10.5 %collective-permute-start.59 = (bf16[36,2,1,512]{3,2,1,0:T(2,128)(2,1)S(1)}, bf16[36,2,1,512]{3,2,1,0:T(2,128)(2,1)S(1)}, u32[]{:S(2)}, u32[]{:S(2)}) collective-permute-start(bf16[36,2,1,512]{3,2,1,0:T(2,128)(2,1)S(1)} %get-tuple-element.148), channel_id=1, source_target_pairs={{1,0},{2,1},{3,2},{4,3},{5,4},{6,5},{7,6},{8,7},{9,8},{10,9},{11,1... | collective-permute-start | bytes 221192 | tf_op jit(solution)/shard_map/ppermute | solution.py:29
  576.4 9.3 %collective-permute-start.60 = (bf16[36,2,1,512]{3,2,1,0:T(2,128)(2,1)S(1)}, bf16[36,2,1,512]{3,2,1,0:T(2,128)(2,1)S(1)}, u32[]{:S(2)}, u32[]{:S(2)}) collective-permute-start(bf16[36,2,1,512]{3,2,1,0:T(2,128)(2,1)S(1)} %get-tuple-element.145), channel_id=1, source_target_pairs={{0,1},{1,2},{2,3},{3,4},{4,5},{5,6},{6,7},{7,8},{8,9},{9,10},{10,1... | collective-permute-start | bytes 221192 | tf_op jit(solution)/shard_map/ppermute | solution.py:28
  588.9 10.2 %collective-permute-start.62 = (bf16[36,2,1,512]{3,2,1,0:T(2,128)(2,1)S(1)}, bf16[36,2,1,512]{3,2,1,0:T(2,128)(2,1)S(1)}, u32[]{:S(2)}, u32[]{:S(2)}) collective-permute-start(bf16[36,2,1,512]{3,2,1,0:T(2,128)(2,1)S(1)} %get-tuple-element.143), channel_id=1, source_target_pairs={{0,1},{1,2},{2,3},{3,4},{4,5},{5,6},{6,7},{7,8},{8,9},{9,10},{10,1... | collective-permute-start | bytes 221192 | tf_op jit(solution)/shard_map/ppermute | solution.py:28
  601.1 9.3 %collective-permute-start.64 = (bf16[36,2,1,512]{3,2,1,0:T(2,128)(2,1)S(1)}, bf16[36,2,1,512]{3,2,1,0:T(2,128)(2,1)S(1)}, u32[]{:S(2)}, u32[]{:S(2)}) collective-permute-start(bf16[36,2,1,512]{3,2,1,0:T(2,128)(2,1)S(1)} %get-tuple-element.141), channel_id=1, source_target_pairs={{0,1},{1,2},{2,3},{3,4},{4,5},{5,6},{6,7},{7,8},{8,9},{9,10},{10,1... | collective-permute-start | bytes 221192 | tf_op jit(solution)/shard_map/ppermute | solution.py:28
  613.2 9.3 %collective-permute-start.66 = (bf16[36,2,1,512]{3,2,1,0:T(2,128)(2,1)S(1)}, bf16[36,2,1,512]{3,2,1,0:T(2,128)(2,1)S(1)}, u32[]{:S(2)}, u32[]{:S(2)}) collective-permute-start(bf16[36,2,1,512]{3,2,1,0:T(2,128)(2,1)S(1)} %get-tuple-element.139), channel_id=1, source_target_pairs={{0,1},{1,2},{2,3},{3,4},{4,5},{5,6},{6,7},{7,8},{8,9},{9,10},{10,1... | collective-permute-start | bytes 221192 | tf_op jit(solution)/shard_map/ppermute | solution.py:28
  700.1 8.8 %collective-permute-start.78 = (bf16[36,2,1,512]{3,2,1,0:T(2,128)(2,1)S(1)}, bf16[36,2,1,512]{3,2,1,0:T(2,128)(2,1)S(1)}, u32[]{:S(2)}, u32[]{:S(2)}) collective-permute-start(bf16[36,2,1,512]{3,2,1,0:T(2,128)(2,1)S(1)} %get-tuple-element.135), channel_id=1, source_target_pairs={{0,1},{1,2},{2,3},{3,4},{4,5},{5,6},{6,7},{7,8},{8,9},{9,10},{10,1... | collective-permute-start | bytes 221192 | tf_op jit(solution)/shard_map/ppermute | solution.py:28
  711.7 9.7 %collective-permute-start.80 = (bf16[36,2,1,512]{3,2,1,0:T(2,128)(2,1)S(1)}, bf16[36,2,1,512]{3,2,1,0:T(2,128)(2,1)S(1)}, u32[]{:S(2)}, u32[]{:S(2)}) collective-permute-start(bf16[36,2,1,512]{3,2,1,0:T(2,128)(2,1)S(1)} %get-tuple-element.133), channel_id=1, source_target_pairs={{0,1},{1,2},{2,3},{3,4},{4,5},{5,6},{6,7},{7,8},{8,9},{9,10},{10,1... | collective-permute-start | bytes 221192 | tf_op jit(solution)/shard_map/ppermute | solution.py:28
  724.1 9.3 %collective-permute-start.82 = (bf16[36,2,1,512]{3,2,1,0:T(2,128)(2,1)S(1)}, bf16[36,2,1,512]{3,2,1,0:T(2,128)(2,1)S(1)}, u32[]{:S(2)}, u32[]{:S(2)}) collective-permute-start(bf16[36,2,1,512]{3,2,1,0:T(2,128)(2,1)S(1)} %get-tuple-element.131), channel_id=1, source_target_pairs={{0,1},{1,2},{2,3},{3,4},{4,5},{5,6},{6,7},{7,8},{8,9},{9,10},{10,1... | collective-permute-start | bytes 221192 | tf_op jit(solution)/shard_map/ppermute | solution.py:28
  726.4 10.5 %collective-permute-start.83 = (bf16[36,2,1,512]{3,2,1,0:T(2,128)(2,1)S(1)}, bf16[36,2,1,512]{3,2,1,0:T(2,128)(2,1)S(1)}, u32[]{:S(2)}, u32[]{:S(2)}) collective-permute-start(bf16[36,2,1,512]{3,2,1,0:T(2,128)(2,1)S(1)} %get-tuple-element.132), channel_id=1, source_target_pairs={{1,0},{2,1},{3,2},{4,3},{5,4},{6,5},{7,6},{8,7},{9,8},{10,9},{11,1... | collective-permute-start | bytes 221192 | tf_op jit(solution)/shard_map/ppermute | solution.py:29
  (65 other events, 423.3 us)
where the time goes:
time: 826 us; the launch traced here: 814 us
  starting transfers between devices  300 us (36%)
  blocking collectives  288 us (35%)
  waiting for transfers between devices  129 us (16%)
  other arithmetic  54.3 us (7%)
  local copies, waits for them, and re-layouts  21.6 us (3%)
  between operations  20.5 us (2%)
    psum x15, blocking collectives, over_axes(): return functools.reduce(lax.psum, axes, x)  218 us
    ppermute x28, starting transfers between devices, extended(): lax.ppermute(leading, axis, [(b, a) for a, b in up])  151 us
    ppermute x28, starting transfers between devices, extended(): lax.ppermute(last, axis, up)  76.7 us
    ppermute x28, waiting for transfers between devices, extended(): lax.ppermute(leading, axis, [(b, a) for a, b in up])  50.7 us
    ppermute x14, waiting for transfers between devices, with_halo(): lax.ppermute(lax.slice_in_dim(block, 0, width, axis=dim), axis, backward)  46.3 us
    ppermute x14, starting transfers between devices, with_halo(): lax.ppermute(lax.slice_in_dim(block, block.shape[dim] - width, None, axis...  44.7 us
    all_to_all x3, blocking collectives, forward(): coarse = lax.all_to_all(coarse, GY, split_axis=2, concat_axis=1, tiled=True)  44.6 us
    ppermute x28, waiting for transfers between devices, extended(): lax.ppermute(last, axis, up)  27 us
  transfers between devices with their start and end apart: 85, of which 71 were waited for; matrix products, arithmetic and copies ran while one was open for 0% of the time, Pallas kernels for 0%

commit v1 on v0

v1 whole, which is shorter than its diff:
```python
import functools

import jax
import jax.numpy as jnp
from jax import lax
from jax.experimental import pallas as pl
from jax.experimental.pallas import tpu as pltpu
from jax.sharding import PartitionSpec as P

TR, TC, FR, FC = 16, 64, 48, 192
HR, HC, ER = 10, 32, 36
PAIRS = ER // 2
NPASS = 4
F32, BF16 = jnp.float32, jnp.bfloat16
MESH = pl.DeviceIdType.MESH
NINE = 1.0 / 9.0


def iota(shape, dim):
    return lax.broadcasted_iota(jnp.int32, shape, dim)


def weight(fine, coarse):
    return jnp.maximum(3 - jnp.abs(fine - 3 * coarse - 1), 0)


def parts(x):
    high = x.astype(BF16)
    rest = x - high.astype(F32)
    mid = rest.astype(BF16)
    low = (rest - mid.astype(F32)).astype(BF16)
    return high, mid, low


def dot_left(const, x):
    return functools.reduce(jnp.add, [jnp.dot(const, p, preferred_element_type=F32) for p in parts(x)])


def dot_right(x, const):
    return functools.reduce(jnp.add, [jnp.dot(p, const, preferred_element_type=F32) for p in parts(x)])


def diffuse(x, q, k, first):
    n = x.shape[0] - 2
    mid = x[1:-1]
    around = (x[2:] + x[:-2]) + (pltpu.roll(mid, 1, 2) + pltpu.roll(mid, 127, 2))
    return q[first + 1 : first + 1 + n] * mid + k[first + 1 : first + 1 + n] * around


def kernel(
    NX, NY, innov, wobs, sscale, source,
    inc_ref, stat_ref,
    mbuf, kbuf, qbuf, ibuf, kc, acc, cbuf, rows_w, cols_w, prows_w, pcols_w,
    snd_c, snd_n, snd_s, rcv_c, rcv_n, rcv_s,
    vq, vb, red_own, red_y, red_own2, red_x,
    m_send, m_recv, m_local, h_send, h_recv, c_send, c_recv, ry_send, ry_recv, rx_send, rx_recv,
):
    gx, gy = lax.axis_index("gx"), lax.axis_index("gy")
    north, south = lax.rem(gx + NX - 1, NX), lax.rem(gx + 1, NX)
    west, east = lax.rem(gy + NY - 1, NY), lax.rem(gy + 1, NY)

    barrier = pltpu.get_barrier_semaphore()
    for d in range(1, NY):
        pl.semaphore_signal(barrier, inc=1, device_id=(gx, lax.rem(gy + d, NY)), device_id_type=MESH)

    def greet(d, _):
        pl.semaphore_signal(barrier, inc=1, device_id=(lax.rem(gx + d, NX), gy), device_id_type=MESH)
        return 0

    lax.fori_loop(1, NX, greet, 0)
    for row in (north, south):
        for col in (west, east):
            pl.semaphore_signal(barrier, inc=1, device_id=(row, col), device_id_type=MESH)

    has_n = jnp.where(gx > 0, 1, 0)
    has_s = jnp.where(gx < NX - 1, 1, 0)
    has_w = jnp.where(gy > 0, 1, 0)
    has_e = jnp.where(gy < NY - 1, 1, 0)
    for b, on in ((0, has_w), (1, 1), (2, has_e)):
        shape = (FC, 128)
        cell = iota(shape, 1) - HC + TC * (b - 1)
        cols_w[:, 128 * b : 128 * (b + 1)] = (weight(iota(shape, 0), cell) * on).astype(F32).astype(BF16)
    for start, count, shift, on in ((0, 24, -2, 1), (48, 16, -2, has_n), (80, 16, 6, has_s)):
        shape = (count, 2 * FR)
        for lev in range(2):
            fine = iota(shape, 1) - FR * lev
            value = jnp.where((fine >= 0) & (fine < FR), weight(fine, iota(shape, 0) + shift) * on, 0)
            rows_w[start + count * lev : start + count * (lev + 1), :] = value.astype(F32)
    shape = (2 * FR, (TR + 2) * 8)
    lev_of = jnp.where(iota(shape, 0) >= FR, 1, 0)
    inner = iota(shape, 1)
    value = jnp.where((inner & 1) == lev_of, weight(iota(shape, 0) - FR * lev_of, (inner >> 3) - 1), 0)
    prows_w[...] = value.astype(F32).astype(BF16)
    shape = (128, FC)
    pcols_w[...] = weight(iota(shape, 1), iota(shape, 0) - HC).astype(F32).astype(BF16)

    def c_copies(app):
        found = []
        for b, col in ((0, west), (1, gy), (2, east)):
            for kind, (row, snd, rcv) in enumerate(((gx, snd_c, rcv_c), (north, snd_n, rcv_n), (south, snd_s, rcv_s))):
                if b == 1 and kind == 0:
                    continue
                found.append(
                    pltpu.make_async_remote_copy(
                        src_ref=snd.at[app, b], dst_ref=rcv.at[app, b],
                        send_sem=c_send.at[app, kind, b], recv_sem=c_recv.at[app, kind, b],
                        device_id=(row, col), device_id_type=MESH,
                    )
                )
        return found

    def restrict(app, v):
        wide = dot_right(v, cols_w[...])
        z = dot_left(rows_w[...].astype(BF16), wide) * NINE
        for b in range(3):
            snd_c[app, b] = z[0:48, 128 * b : 128 * (b + 1)]
            snd_n[app, b] = z[48:80, 128 * b : 128 * (b + 1)]
            snd_s[app, b] = z[80:112, 128 * b : 128 * (b + 1)]

    first = wobs[...] * innov[...]
    vq[0] = first
    restrict(0, first)

    pl.semaphore_wait(barrier, (NY - 1) + (NX - 1) + 4)

    for copy in c_copies(0):
        copy.start()

    moves = []
    for d in range(1, NY):
        col = lax.rem(gy + d, NY)
        moves.append(
            pltpu.make_async_remote_copy(
                src_ref=source.at[col], dst_ref=mbuf.at[gy + 5],
                send_sem=m_send.at[d], recv_sem=m_recv.at[d],
                device_id=(gx, col), device_id_type=MESH,
            )
        )
    for copy in moves:
        copy.start()
    own = pltpu.make_async_copy(source.at[gy], mbuf.at[gy + 5], m_local)
    own.start()
    own.wait()
    for copy in moves:
        copy.wait_recv()
    halos = [
        pltpu.make_async_remote_copy(
            src_ref=mbuf.at[pl.ds(begin, 5)], dst_ref=mbuf.at[pl.ds(to, 5)],
            send_sem=h_send.at[i], recv_sem=h_recv.at[i], device_id=(row, gy), device_id_type=MESH,
        )
        for i, (begin, to, row) in enumerate(((5, 13, north), (8, 0, south)))
    ]
    for copy in halos:
        copy.start()
    for copy in halos:
        copy.wait_recv()

    row_of = iota((ER, 8, 128), 0)
    inside = jnp.where(((row_of >= HR) | (gx > 0)) & ((row_of < HR + TR) | (gx < NX - 1)), 1.0, 0.0)
    rate = mbuf[:, 9].astype(F32).reshape(ER, 8, 128) * inside
    kbuf[...] = rate
    qbuf[...] = 1.0 - 4.0 * rate
    ibuf[...] = jnp.where(rate > 0.0, 1.0 / jnp.where(rate > 0.0, rate, 1.0), 0.0)

    lev_odd = (iota((8, 128), 0) & 1) == 1

    def apply(app, v):
        for copy in c_copies(app):
            copy.wait_recv()
        mine = snd_c[app, 1] + rcv_c[app, 0] + rcv_c[app, 2]
        north_in = rcv_s[app, 0] + rcv_s[app, 1] + rcv_s[app, 2]
        south_in = rcv_n[app, 0] + rcv_n[app, 1] + rcv_n[app, 2]
        for lev in range(2):
            c, n, s = mine[24 * lev : 24 * lev + 24], north_in[16 * lev : 16 * lev + 16], south_in[16 * lev : 16 * lev + 16]
            cbuf[lev, 0:8] = n[0:8]
            cbuf[lev, 8:16] = n[8:16] + c[0:8]
            cbuf[lev, 16:24] = c[8:16]
            cbuf[lev, 24:32] = c[16:24] + s[0:8]
            cbuf[lev, 32:40] = s[8:16]
        for e in range(1, ER - 1):
            even = jnp.broadcast_to(cbuf[0, e : e + 1, :], (8, 128))
            odd = jnp.broadcast_to(cbuf[1, e : e + 1, :], (8, 128))
            kc[e] = jnp.where(lev_odd, odd, even) * kbuf[e]
        acc[...] = jnp.zeros_like(acc)

        def chunk(ch, _):
            m = mbuf[:, ch].astype(F32).reshape(ER, 8, 128)
            x = m[1 : ER - 1] * kc[1 : ER - 1]
            at = 1
            for repeat in range(NPASS):
                x = diffuse(x, qbuf, kbuf, at)
                at += 1
            x = x * ibuf[at : at + x.shape[0]]
            for repeat in range(NPASS):
                x = diffuse(x, qbuf, kbuf, at)
                at += 1
            acc[...] += x * m[at : ER - at]
            return 0

        lax.fori_loop(0, 9, chunk, 0)
        tall = dot_left(prows_w[...], acc[...].reshape((TR + 2) * 8, 128))
        scale = sscale[...]
        return scale * scale * v + dot_right(tall, pcols_w[...]) * NINE

    lane = iota((1, 128), 1)

    def pack(pairs):
        out = jnp.zeros((1, 128), F32)
        for i, (left, right) in enumerate(pairs):
            total = jnp.sum(jnp.sum(left * right, axis=0, keepdims=True), axis=1, keepdims=True)
            out = jnp.where(lane == i, total, out)
        return out

    def y_copy(use, d):
        return pltpu.make_async_remote_copy(
            src_ref=red_own.at[use], dst_ref=red_y.at[use, d], send_sem=ry_send.at[use, d], recv_sem=ry_recv.at[use, d],
            device_id=(gx, lax.rem(gy + d, NY)), device_id_type=MESH,
        )

    def x_copy(use, d):
        return pltpu.make_async_remote_copy(
            src_ref=red_own2.at[use], dst_ref=red_x.at[use, d], send_sem=rx_send.at[use, d], recv_sem=rx_recv.at[use, d],
            device_id=(lax.rem(gx + d, NX), gy), device_id_type=MESH,
        )

    def each(count, make, what):
        def body(d, _):
            getattr(make(d), what)()
            return 0

        lax.fori_loop(1, count, body, 0)

    def reduce_start(use, row):
        red_own[use] = row
        each(NY, functools.partial(y_copy, use), "start")

    def reduce_middle(use):
        each(NY, functools.partial(y_copy, use), "wait_recv")
        total = red_own[use]
        for d in range(1, NY):
            total = total + red_y[use, d]
        red_own2[use] = total
        each(NX, functools.partial(x_copy, use), "start")

    def reduce_end(use):
        each(NX, functools.partial(x_copy, use), "wait_recv")
        total = red_own2[use]
        for d in range(1, NX):
            total = total + red_x[use, d]
        each(NY, functools.partial(y_copy, use), "wait_send")
        each(NX, functools.partial(x_copy, use), "wait_send")
        return total

    def pick(row, i):
        return jnp.sum(jnp.where(lane == i, row, 0.0), axis=1, keepdims=True)

    w = wobs[...]
    b0 = apply(0, vq[0])
    vb[0] = b0
    q1 = w * b0
    restrict(1, q1)
    for copy in c_copies(1):
        copy.start()
    reduce_start(0, pack(((vq[0], b0), (q1, b0))))
    vq[1] = q1
    reduce_middle(0)
    b1 = apply(1, vq[1])
    sums = reduce_end(0)
    theta = pick(sums, 1) / pick(sums, 0)
    b1 = b1 - theta * vb[0]
    vq[1] = vq[1] - theta * vq[0]
    vb[1] = b1
    q2 = w * b1
    restrict(2, q2)
    for copy in c_copies(2):
        copy.start()
    vq[2] = q2
    b2 = apply(2, vq[2])
    vb[2] = b2
    q0, q1, b0, b1 = vq[0], vq[1], vb[0], vb[1]
    wb = (w * b0, w * b1, w * b2)
    q2 = vq[2]
    row = pack((
        (q0, b0), (q0, b1), (q0, b2), (q1, b1), (q1, b2), (q2, b2),
        (b0, wb[0]), (b0, wb[1]), (b0, wb[2]), (b1, wb[1]), (b1, wb[2]), (b2, wb[2]),
    ))
    reduce_start(1, row)
    reduce_middle(1)
    sums = reduce_end(1)
    e = [pick(sums, i) for i in range(12)]
    s00, s01, s02, s11, s12, s22 = [e[i] + e[6 + i] for i in range(6)]
    tiny = 1e-7
    i0 = 1.0 / s00
    l10, l20 = s01 * i0, s02 * i0
    d1 = s11 - l10 * s01
    i1 = jnp.where(d1 > tiny * s11, 1.0 / d1, 0.0)
    t12 = s12 - l10 * s02
    l21 = t12 * i1
    d2 = s22 - l20 * s02 - l21 * t12
    i2 = jnp.where(d2 > tiny * s22, 1.0 / d2, 0.0)
    r0, r1, r2 = e[0], e[1], e[2]
    r1 = r1 - l10 * r0
    r2 = r2 - l20 * r0 - l21 * r1
    z2 = r2 * i2
    z1 = r1 * i1 - l21 * z2
    z0 = r0 * i0 - l10 * z1 - l20 * z2
    inc_ref[...] = z0 * vb[0] + z1 * vb[1] + z2 * vb[2]
    stat_ref[...] = sscale[...] * (z0 * vq[0] + z1 * vq[1] + z2 * vq[2])

    for app in range(3):
        for copy in c_copies(app):
            copy.wait_send()
    for copy in moves:
        copy.wait_send()
    for copy in halos:
        copy.wait_send()


def per_device(NX, NY, innovation, obs_weight, static_scale, members, diffusivity):
    wide = members.shape[-1]
    m = members.reshape(9, 4, 2, 2, wide).transpose(0, 3, 1, 2, 4).reshape(9, 16, wide)
    k = jnp.broadcast_to(diffusivity.transpose(1, 0, 2)[:, None], (2, 4, 2, wide)).reshape(1, 16, wide)
    both = jnp.pad(jnp.concatenate([m, k]), ((0, 0), (0, 0), (HC, 128 - TC - HC)))
    source = jnp.stack([both[:, :, TC * j : TC * j + 128] for j in range(NY)])
    vec = (2 * FR, FC)
    vmem = pl.BlockSpec(memory_space=pltpu.VMEM)
    dma = pltpu.SemaphoreType.DMA
    inc, stat = pl.pallas_call(
        functools.partial(kernel, NX, NY),
        out_shape=(jax.ShapeDtypeStruct(vec, F32), jax.ShapeDtypeStruct(vec, F32)),
        in_specs=[vmem] * 4,
        out_specs=(vmem, vmem),
        scratch_shapes=[
            pltpu.VMEM((PAIRS, 10, 16, 128), BF16),
            pltpu.VMEM((ER, 8, 128), F32),
            pltpu.VMEM((ER, 8, 128), F32),
            pltpu.VMEM((ER, 8, 128), F32),
            pltpu.VMEM((ER, 8, 128), F32),
            pltpu.VMEM((TR + 2, 8, 128), F32),
            pltpu.VMEM((2, 40, 128), F32),
            pltpu.VMEM((112, 2 * FR), F32),
            pltpu.VMEM((FC, 384), BF16),
            pltpu.VMEM((2 * FR, (TR + 2) * 8), BF16),
            pltpu.VMEM((128, FC), BF16),
            pltpu.VMEM((3, 3, 48, 128), F32),
            pltpu.VMEM((3, 3, 32, 128), F32),
            pltpu.VMEM((3, 3, 32, 128), F32),
            pltpu.VMEM((3, 3, 48, 128), F32),
            pltpu.VMEM((3, 3, 32, 128), F32),
            pltpu.VMEM((3, 3, 32, 128), F32),
            pltpu.VMEM((3,) + vec, F32),
            pltpu.VMEM((3,) + vec, F32),
            pltpu.VMEM((2, 1, 128), F32),
            pltpu.VMEM((2, NY, 1, 128), F32),
            pltpu.VMEM((2, 1, 128), F32),
            pltpu.VMEM((2, NX, 1, 128), F32),
            dma((NY,)), dma((NY,)), dma,
            dma((2,)), dma((2,)),
            dma((3, 3, 3)), dma((3, 3, 3)),
            dma((2, NY)), dma((2, NY)),
            dma((2, NX)), dma((2, NX)),
        ],
        compiler_params=pltpu.CompilerParams(collective_id=0, has_side_effects=True),
        name="solve",
    )(innovation.reshape(vec), obs_weight.reshape(vec), static_scale.reshape(vec), source)
    return inc.reshape(2, FR, FC), stat.reshape(2, FR, FC)


def solution(mesh):
    NX, NY = mesh.shape["gx"], mesh.shape["gy"]
    fine = P(None, "gx", "gy")
    return jax.shard_map(
        functools.partial(per_device, NX, NY),
        mesh=mesh,
        in_specs=(fine, fine, fine, P(None, None, ("gx", "gy"), None), P(None, ("gx", "gy"), None)),
        out_specs=(fine, fine),
        check_vma=False,
    )
```

time: 826 us -> 86.1 us (0.10); the launches traced: 814 us -> 85.9 us
  starting transfers between devices: 300 us -> 0 us
  blocking collectives: 288 us -> 0 us
  waiting for transfers between devices: 129 us -> 0 us
  Pallas kernels: 0 us -> 79.7 us
  other arithmetic: 54.3 us -> 0 us
  between operations: 20.5 us -> 0.72 us
  local copies, waits for them, and re-layouts: 21.6 us -> 5.48 us
    ppermute x84 -> x0, starting transfers between devices: 295 us -> none  [the longest x28 151 us: extended(): lax.ppermute(leading, axis, [(b, a) for a, b in up])]
    psum x15 -> x0, blocking collectives: 218 us -> none  [over_axes(): return functools.reduce(lax.psum, axes, x)]
    ppermute x84 -> x0, waiting for transfers between devices: 124 us -> none  [the longest x28 50.7 us: extended(): lax.ppermute(leading, axis, [(b, a) for a, b in up])]
    pallas_call x0 -> x1, Pallas kernels: none -> 79.7 us  [per_device(): pl.pallas_call(functools.partial(kernel, NX, NY), out_shape=(jax.ShapeDty...]
    all_to_all x6 -> x0, blocking collectives: 70.2 us -> none  [the longest x3 44.6 us: forward(): coarse = lax.all_to_all(coarse, GY, split_axis=2, concat_axis=1, tiled=True)]
    convert_element_type x57 -> x0, other arithmetic: 34.2 us -> none  [the longest x28 21.3 us: widen(): values.astype(jnp.bfloat16)]
    slice x86 -> x0, local copies, waits for them, and re-layouts: 10.1 us -> none  [the longest x28 5.84 us: extended(): last = lax.slice_in_dim(x, length - width, length, axis=dim)]
    reduce_sum x9 -> x0, other arithmetic: 10.1 us -> none  [the longest x6 7.06 us: inner(): return jnp.sum(left[0] * right[0]) + jnp.sum(left[1] * right[1])]
  transfers between devices with their start and end apart: 85 -> 0, of which waited for: 71 -> 0; matrix products, arithmetic and copies ran while one was open for 0% -> 0% of each run, Pallas kernels for 0% -> 0%
where the time goes in v1:
time: 86.1 us; the launch traced here: 85.9 us
  Pallas kernels  79.7 us (93%)
  local copies, waits for them, and re-layouts  5.48 us (6%)
    pallas_call x1, Pallas kernels, per_device(): pl.pallas_call(functools.partial(kernel, NX, NY), out_shape=(jax.ShapeDty...  79.7 us
    unnamed x16, local copies, waits for them, and re-layouts  4.26 us

profile of v1, /device:TPU:1, one launch (start us, length us, event | category | flops | bytes accessed | tf_op | source)
XLA Modules:
  0.0 85.9 jit_solution(7523505157649829756)
XLA Ops:
  0.6 0.0 copy-start.2
  0.6 0.7 copy-done.2
  1.4 1.0 %copy.10 = bf16[9,4,2,2,512]{4,2,1,3,0:T(2,128)(2,1)S(1)} copy(bf16[9,4,2,2,512]{4,3,2,1,0:T(2,128)(2,1)} %bitcast.43) | data formatting | bytes 294912 | tf_op jit(solution)/shard_map/reshape | solution.py:321
  2.4 0.1 reshape.33
  2.5 0.1 fusion.1
  2.6 0.1 fusion.9
  2.7 0.1 fusion.8
  2.8 0.1 fusion.7
  2.9 0.1 fusion.6
  3.0 0.1 fusion.5
  3.1 0.1 fusion.4
  3.2 0.1 fusion.3.source
  3.2 0.0 copy-start
  3.3 0.7 copy-done
  4.0 79.7 %solve.1 = (f32[96,192]{1,0:T(8,128)}, f32[96,192]{1,0:T(8,128)}) custom-call(f32[96,192]{1,0:T(8,128)} %bitcast.44, f32[96,192]{1,0:T(8,128)} %bitcast.45, f32[96,192]{1,0:T(8,128)} %bitcast.46, bf16[8,10,16,128]{3,2,1,0:T(8,128)(2,1)} %copy-done), custom_call_target="tpu_custom_call" | custom-call | tf_op jit(solution)/shard_map/solve/pallas_call | solution.py:328
  83.7 0.0 copy-start.1
  83.7 1.6 %copy.21 = f32[2,48,192]{2,1,0:T(8,128)} copy(f32[2,48,192]{2,1,0:T(8,128)} %bitcast.48) | data formatting | bytes 147456
  85.3 0.0 copy-done.1
  85.3 0.6 copy.22
  (5 shorter events, 0.0 us)
Async XLA Ops:
  0.6 0.7 copy-start.2
  3.2 0.7 copy-start
  83.7 1.6 %copy-start.1 = (f32[96,192]{1,0:T(8,128)S(1)}, f32[96,192]{1,0:T(8,128)}, u32[]{:S(2)}) copy-start(f32[96,192]{1,0:T(8,128)} %get-tuple-element.5) | copy-start | bytes 221188

commit v2 on v1

--- a/solution.py
+++ b/solution.py
@@ -40,17 +40,19 @@
     return functools.reduce(jnp.add, [jnp.dot(p, const, preferred_element_type=F32) for p in parts(x)])
 
 
-def diffuse(x, q, k, first):
-    n = x.shape[0] - 2
-    mid = x[1:-1]
-    around = (x[2:] + x[:-2]) + (pltpu.roll(mid, 1, 2) + pltpu.roll(mid, 127, 2))
-    return q[first + 1 : first + 1 + n] * mid + k[first + 1 : first + 1 + n] * around
+def diffuse(row, store, center, around, first, last):
+    above, here = row(first - 1), row(first)
+    for r in range(first, last):
+        below = row(r + 1)
+        near = (above + below) + (pltpu.roll(here, 1, 2) + pltpu.roll(here, 127, 2))
+        store(r, center[r][None] * here + around[r][None] * near)
+        above, here = here, below
 
 
 def kernel(
     NX, NY, innov, wobs, sscale, source,
     inc_ref, stat_ref,
-    mbuf, kbuf, qbuf, ibuf, kc, acc, cbuf, rows_w, cols_w, prows_w, pcols_w,
+    mbuf, mf, xa, xb, kbuf, qbuf, ibuf, rbuf, kc, acc, cbuf, rows_w, cols_w, prows_w, pcols_w,
     snd_c, snd_n, snd_s, rcv_c, rcv_n, rcv_s,
     vq, vb, red_own, red_y, red_own2, red_x,
     m_send, m_recv, m_local, h_send, h_recv, c_send, c_recv, ry_send, ry_recv, rx_send, rx_recv,
@@ -140,27 +142,42 @@
         copy.start()
     own = pltpu.make_async_copy(source.at[gy], mbuf.at[gy + 5], m_local)
     own.start()
+
+    def halo(side, d):
+        g = lax.rem(gy + NY - d, NY)
+        return g <= 4 if side == 0 else g >= 3, pltpu.make_async_remote_copy(
+            src_ref=source.at[gy] if d == 0 else mbuf.at[g + 5],
+            dst_ref=mbuf.at[jnp.minimum(g, 4) + 13 if side == 0 else jnp.maximum(g, 3) - 3],
+            send_sem=h_send.at[side, d], recv_sem=h_recv.at[side, d],
+            device_id=(north if side == 0 else south, gy), device_id_type=MESH,
+        )
+
+    def halo_do(d, what):
+        for side in range(2):
+            used, copy = halo(side, d)
+
+            @pl.when(used)
+            def _():
+                getattr(copy, what)()
+
+    halo_do(0, "start")
+    for d in range(1, NY):
+        moves[d - 1].wait_recv()
+        halo_do(d, "start")
     own.wait()
-    for copy in moves:
-        copy.wait_recv()
-    halos = [
-        pltpu.make_async_remote_copy(
-            src_ref=mbuf.at[pl.ds(begin, 5)], dst_ref=mbuf.at[pl.ds(to, 5)],
-            send_sem=h_send.at[i], recv_sem=h_recv.at[i], device_id=(row, gy), device_id_type=MESH,
-        )
-        for i, (begin, to, row) in enumerate(((5, 13, north), (8, 0, south)))
-    ]
-    for copy in halos:
-        copy.start()
-    for copy in halos:
-        copy.wait_recv()
+    for d in range(NY):
+        halo_do(d, "wait_recv")
 
     row_of = iota((ER, 8, 128), 0)
     inside = jnp.where(((row_of >= HR) | (gx > 0)) & ((row_of < HR + TR) | (gx < NX - 1)), 1.0, 0.0)
     rate = mbuf[:, 9].astype(F32).reshape(ER, 8, 128) * inside
     kbuf[...] = rate
     qbuf[...] = 1.0 - 4.0 * rate
-    ibuf[...] = jnp.where(rate > 0.0, 1.0 / jnp.where(rate > 0.0, rate, 1.0), 0.0)
+    known = rate > 0.0
+    ibuf[...] = jnp.where(known, 1.0, 0.0)
+    rbuf[...] = jnp.where(known, 1.0 / jnp.where(known, rate, 1.0) - 4.0, 0.0)
+    for ch in range(9):
+        mf[:, ch] = mbuf[:, ch].astype(F32).reshape(ER, 8, 128)
 
     lev_odd = (iota((8, 128), 0) & 1) == 1
 
@@ -181,23 +198,19 @@
             even = jnp.broadcast_to(cbuf[0, e : e + 1, :], (8, 128))
             odd = jnp.broadcast_to(cbuf[1, e : e + 1, :], (8, 128))
             kc[e] = jnp.where(lev_odd, odd, even) * kbuf[e]
-        acc[...] = jnp.zeros_like(acc)
-
-        def chunk(ch, _):
-            m = mbuf[:, ch].astype(F32).reshape(ER, 8, 128)
-            x = m[1 : ER - 1] * kc[1 : ER - 1]
-            at = 1
-            for repeat in range(NPASS):
-                x = diffuse(x, qbuf, kbuf, at)
-                at += 1
-            x = x * ibuf[at : at + x.shape[0]]
-            for repeat in range(NPASS):
-                x = diffuse(x, qbuf, kbuf, at)
-                at += 1
-            acc[...] += x * m[at : ER - at]
-            return 0
-
-        lax.fori_loop(0, 9, chunk, 0)
+        bufs = (xa, xb)
+        for p in range(2 * NPASS):
+            src, dst = bufs[p % 2], bufs[(p + 1) % 2]
+            row = (lambda r: mf[r] * kc[r][None]) if p == 0 else (lambda r, src=src: src[r])
+
+            def store(r, x, dst=dst, p=p):
+                if p == 2 * NPASS - 1:
+                    acc[r - (HR - 1)] = jnp.sum(x * mf[r], axis=0)
+                else:
+                    dst[r] = x
+
+            middle = p == NPASS - 1
+            diffuse(row, store, rbuf if middle else qbuf, ibuf if middle else kbuf, 2 + p, ER - 2 - p)
         tall = dot_left(prows_w[...], acc[...].reshape((TR + 2) * 8, 128))
         scale = sscale[...]
         return scale * scale * v + dot_right(tall, pcols_w[...]) * NINE
@@ -312,8 +325,8 @@
             copy.wait_send()
     for copy in moves:
         copy.wait_send()
-    for copy in halos:
-        copy.wait_send()
+    for d in range(NY):
+        halo_do(d, "wait_send")
 
 
 def per_device(NX, NY, innovation, obs_weight, static_scale, members, diffusivity):
@@ -332,6 +345,10 @@
         out_specs=(vmem, vmem),
         scratch_shapes=[
             pltpu.VMEM((PAIRS, 10, 16, 128), BF16),
+            pltpu.VMEM((ER, 9, 8, 128), F32),
+            pltpu.VMEM((ER, 9, 8, 128), F32),
+            pltpu.VMEM((ER, 9, 8, 128), F32),
+            pltpu.VMEM((ER, 8, 128), F32),
             pltpu.VMEM((ER, 8, 128), F32),
             pltpu.VMEM((ER, 8, 128), F32),
             pltpu.VMEM((ER, 8, 128), F32),
@@ -355,7 +372,7 @@
             pltpu.VMEM((2, 1, 128), F32),
             pltpu.VMEM((2, NX, 1, 128), F32),
             dma((NY,)), dma((NY,)), dma,
-            dma((2,)), dma((2,)),
+            dma((2, NY)), dma((2, NY)),
             dma((3, 3, 3)), dma((3, 3, 3)),
             dma((2, NY)), dma((2, NY)),
             dma((2, NX)), dma((2, NX)),

time: 86.1 us -> 74.9 us (0.87)
  Pallas kernels: 79.7 us -> 68.5 us
    pallas_call x1, Pallas kernels: 79.7 us -> 68.5 us  [per_device(): pl.pallas_call(functools.partial(kernel, NX, NY), out_shape=(jax.ShapeDty...]
where the time goes in v2:
time: 74.9 us; the launch traced here: 74.7 us
  Pallas kernels  68.5 us (91%)
  local copies, waits for them, and re-layouts  5.48 us (7%)
    pallas_call x1, Pallas kernels, per_device(): pl.pallas_call(functools.partial(kernel, NX, NY), out_shape=(jax.ShapeDty...  68.5 us
    unnamed x16, local copies, waits for them, and re-layouts  4.26 us

profile of v2, /device:TPU:1, one launch (start us, length us, event | category | flops | bytes accessed | tf_op | source)
XLA Modules:
  0.0 74.7 jit_solution(13400353170742290619)
XLA Ops:
  0.6 0.0 copy-start.2
  0.6 0.7 copy-done.2
  1.4 1.0 %copy.10 = bf16[9,4,2,2,512]{4,2,1,3,0:T(2,128)(2,1)S(1)} copy(bf16[9,4,2,2,512]{4,3,2,1,0:T(2,128)(2,1)} %bitcast.43) | data formatting | bytes 294912 | tf_op jit(solution)/shard_map/reshape | solution.py:334
  2.4 0.1 reshape.33
  2.5 0.1 fusion.1
  2.6 0.1 fusion.9
  2.7 0.1 fusion.8
  2.8 0.1 fusion.7
  2.9 0.1 fusion.6
  3.0 0.1 fusion.5
  3.1 0.1 fusion.4
  3.2 0.1 fusion.3.source
  3.2 0.0 copy-start
  3.3 0.7 copy-done
  4.0 68.5 %solve.1 = (f32[96,192]{1,0:T(8,128)}, f32[96,192]{1,0:T(8,128)}) custom-call(f32[96,192]{1,0:T(8,128)} %bitcast.44, f32[96,192]{1,0:T(8,128)} %bitcast.45, f32[96,192]{1,0:T(8,128)} %bitcast.46, bf16[8,10,16,128]{3,2,1,0:T(8,128)(2,1)} %copy-done), custom_call_target="tpu_custom_call" | custom-call | tf_op jit(solution)/shard_map/solve/pallas_call | solution.py:341
  72.5 0.0 copy-start.1
  72.5 1.6 %copy.21 = f32[2,48,192]{2,1,0:T(8,128)} copy(f32[2,48,192]{2,1,0:T(8,128)} %bitcast.48) | data formatting | bytes 147456
  74.1 0.0 copy-done.1
  74.1 0.6 copy.22
  (5 shorter events, 0.0 us)
Async XLA Ops:
  0.6 0.7 copy-start.2
  3.2 0.7 copy-start
  72.5 1.6 %copy-start.1 = (f32[96,192]{1,0:T(8,128)S(1)}, f32[96,192]{1,0:T(8,128)}, u32[]{:S(2)}) copy-start(f32[96,192]{1,0:T(8,128)} %get-tuple-element.5) | copy-start | bytes 221188

commit v3 on v2

--- a/solution.py
+++ b/solution.py
@@ -8,7 +8,8 @@
 from jax.sharding import PartitionSpec as P
 
 TR, TC, FR, FC = 16, 64, 48, 192
-HR, HC, ER = 10, 32, 36
+HR, HC, ER, POS = 10, 9, 36, 28
+MSG = 112
 PAIRS = ER // 2
 NPASS = 4
 F32, BF16 = jnp.float32, jnp.bfloat16
@@ -44,15 +45,19 @@
     above, here = row(first - 1), row(first)
     for r in range(first, last):
         below = row(r + 1)
-        near = (above + below) + (pltpu.roll(here, 1, 2) + pltpu.roll(here, 127, 2))
-        store(r, center[r][None] * here + around[r][None] * near)
+        for p in range(3):
+            before = here[p - 1] if p else pltpu.roll(here[2], 1, 2)
+            after = here[p + 1] if p < 2 else pltpu.roll(here[0], 127, 2)
+            near = (above[p] + below[p]) + (before + after)
+            store(r, p, center[r, p][None] * here[p] + around[r, p][None] * near)
         above, here = here, below
 
 
 def kernel(
-    NX, NY, innov, wobs, sscale, source,
+    NX, NY, innov, wobs, sscale, raw,
     inc_ref, stat_ref,
-    mbuf, mf, xa, xb, kbuf, qbuf, ibuf, rbuf, kc, acc, cbuf, rows_w, cols_w, prows_w, pcols_w,
+    mbuf, mf, xa, xb, kbuf, qbuf, ibuf, rbuf, kc, acc, cbuf, cw, kw, kcomp, stage, source, unpacked,
+    rows_w, cols_w, prows_w, pcols_w, spread_w,
     snd_c, snd_n, snd_s, rcv_c, rcv_n, rcv_s,
     vq, vb, red_own, red_y, red_own2, red_x,
     m_send, m_recv, m_local, h_send, h_recv, c_send, c_recv, ry_send, ry_recv, rx_send, rx_recv,
@@ -62,17 +67,13 @@
     west, east = lax.rem(gy + NY - 1, NY), lax.rem(gy + 1, NY)
 
     barrier = pltpu.get_barrier_semaphore()
-    for d in range(1, NY):
-        pl.semaphore_signal(barrier, inc=1, device_id=(gx, lax.rem(gy + d, NY)), device_id_type=MESH)
-
-    def greet(d, _):
+    for d in sorted(range(1, NX), key=lambda d: min(d % 8, 8 - d % 8), reverse=True):
         pl.semaphore_signal(barrier, inc=1, device_id=(lax.rem(gx + d, NX), gy), device_id_type=MESH)
-        return 0
-
-    lax.fori_loop(1, NX, greet, 0)
     for row in (north, south):
         for col in (west, east):
             pl.semaphore_signal(barrier, inc=1, device_id=(row, col), device_id_type=MESH)
+    for d in range(1, NY):
+        pl.semaphore_signal(barrier, inc=1, device_id=(gx, lax.rem(gy + d, NY)), device_id_type=MESH)
 
     has_n = jnp.where(gx > 0, 1, 0)
     has_s = jnp.where(gx < NX - 1, 1, 0)
@@ -80,8 +81,10 @@
     has_e = jnp.where(gy < NY - 1, 1, 0)
     for b, on in ((0, has_w), (1, 1), (2, has_e)):
         shape = (FC, 128)
-        cell = iota(shape, 1) - HC + TC * (b - 1)
-        cols_w[:, 128 * b : 128 * (b + 1)] = (weight(iota(shape, 0), cell) * on).astype(F32).astype(BF16)
+        at = iota(shape, 1)
+        cell = 3 * (at & 31) + (at >> 5) - HC + TC * (b - 1)
+        value = jnp.where(((at & 31) < POS) & (at < 96), weight(iota(shape, 0), cell) * on, 0)
+        cols_w[:, 128 * b : 128 * (b + 1)] = value.astype(F32).astype(BF16)
     for start, count, shift, on in ((0, 24, -2, 1), (48, 16, -2, has_n), (80, 16, 6, has_s)):
         shape = (count, 2 * FR)
         for lev in range(2):
@@ -93,8 +96,15 @@
     inner = iota(shape, 1)
     value = jnp.where((inner & 1) == lev_of, weight(iota(shape, 0) - FR * lev_of, (inner >> 3) - 1), 0)
     prows_w[...] = value.astype(F32).astype(BF16)
-    shape = (128, FC)
-    pcols_w[...] = weight(iota(shape, 1), iota(shape, 0) - HC).astype(F32).astype(BF16)
+    for p in range(3):
+        shape = (128, FC)
+        at = iota(shape, 0) & 31
+        value = jnp.where(at < POS, weight(iota(shape, 1), 3 * at + p - HC), 0)
+        pcols_w[128 * p : 128 * (p + 1)] = value.astype(F32).astype(BF16)
+        shape = (128, 128)
+        at = iota(shape, 1) & 31
+        value = jnp.where((at < POS) & (iota(shape, 0) == 32 * p + at), 1, 0)
+        spread_w[:, 128 * p : 128 * (p + 1)] = value.astype(F32).astype(BF16)
 
     def c_copies(app):
         found = []
@@ -123,6 +133,28 @@
     vq[0] = first
     restrict(0, first)
 
+    group = iota((24, 128), 1) >> 5
+    for odd in range(2):
+        shape = (256, 128)
+        at = iota(shape, 1)
+        from_lane = (128 * (1 - odd) + TC * odd - HC) + 3 * (at & 31) + (at >> 5)
+        value = jnp.where(((at & 31) < POS) & (at < 96) & (iota(shape, 0) == from_lane), 1, 0)
+        select = value.astype(F32).astype(BF16)
+        for j in range(odd, NY, 2):
+            lane = 128 * ((j + 1) // 2)
+            cut = jnp.dot(raw[:, lane : lane + 256], select, preferred_element_type=F32)
+            for row in range(2):
+                for p in range(3):
+                    x = jnp.zeros((24, 128), F32)
+                    for g in range(4):
+                        piece = cut[24 * (2 * g + row) : 24 * (2 * g + row + 1)]
+                        turn = (32 * (g - p)) % 128
+                        x = jnp.where(group == g, pltpu.roll(piece, turn, 1) if turn else piece, x)
+                    start = 18 * (3 * row + p)
+                    stage[j, start : start + 24] = x
+            stage[j, MSG - 4 : MSG] = cut[192:196]
+            source[j] = stage[j, 0:MSG].astype(BF16)
+
     pl.semaphore_wait(barrier, (NY - 1) + (NX - 1) + 4)
 
     for copy in c_copies(0):
@@ -165,21 +197,43 @@
         moves[d - 1].wait_recv()
         halo_do(d, "start")
     own.wait()
+
+    def unpack(pair):
+        unpacked[pair, 0:MSG] = mbuf[pair].astype(F32)
+        real = iota((24, 128), 0) < 18
+        for row in range(2):
+            for p in range(3):
+                start = 18 * (3 * row + p)
+                x = jnp.where(real, unpacked[pair, start : start + 24], 0.0)
+                mf[2 * pair + row, p] = x.reshape(3, 8, 128)
+        kcomp[4 * pair : 4 * pair + 4] = unpacked[pair, MSG - 4 : MSG]
+
+    for pair in range(5, 13):
+        unpack(pair)
     for d in range(NY):
         halo_do(d, "wait_recv")
-
-    row_of = iota((ER, 8, 128), 0)
-    inside = jnp.where(((row_of >= HR) | (gx > 0)) & ((row_of < HR + TR) | (gx < NX - 1)), 1.0, 0.0)
-    rate = mbuf[:, 9].astype(F32).reshape(ER, 8, 128) * inside
-    kbuf[...] = rate
-    qbuf[...] = 1.0 - 4.0 * rate
-    known = rate > 0.0
-    ibuf[...] = jnp.where(known, 1.0, 0.0)
-    rbuf[...] = jnp.where(known, 1.0 / jnp.where(known, rate, 1.0) - 4.0, 0.0)
-    for ch in range(9):
-        mf[:, ch] = mbuf[:, ch].astype(F32).reshape(ER, 8, 128)
+    for pair in (0, 1, 2, 3, 4, 13, 14, 15, 16, 17):
+        unpack(pair)
 
     lev_odd = (iota((8, 128), 0) & 1) == 1
+    kw[...] = jnp.dot(kcomp[...].astype(BF16), spread_w[...], preferred_element_type=F32)
+
+    def by_level(ref, even, odd, p):
+        lanes = slice(128 * p, 128 * (p + 1))
+        return jnp.where(
+            lev_odd, jnp.broadcast_to(ref[odd : odd + 1, lanes], (8, 128)), jnp.broadcast_to(ref[even : even + 1, lanes], (8, 128))
+        )
+
+    on_n, on_s = jnp.where(gx > 0, 1.0, 0.0), jnp.where(gx < NX - 1, 1.0, 0.0)
+    for e in range(ER):
+        for p in range(3):
+            rate = by_level(kw, 2 * e, 2 * e + 1, p)
+            rate = rate * (on_n if e < HR else on_s if e >= HR + TR else 1.0)
+            known = rate > 0.0
+            kbuf[e, p] = rate
+            qbuf[e, p] = 1.0 - 4.0 * rate
+            ibuf[e, p] = jnp.where(known, 1.0, 0.0)
+            rbuf[e, p] = jnp.where(known, 1.0 / jnp.where(known, rate, 1.0) - 4.0, 0.0)
 
     def apply(app, v):
         for copy in c_copies(app):
@@ -189,29 +243,32 @@
         south_in = rcv_n[app, 0] + rcv_n[app, 1] + rcv_n[app, 2]
         for lev in range(2):
             c, n, s = mine[24 * lev : 24 * lev + 24], north_in[16 * lev : 16 * lev + 16], south_in[16 * lev : 16 * lev + 16]
-            cbuf[lev, 0:8] = n[0:8]
-            cbuf[lev, 8:16] = n[8:16] + c[0:8]
-            cbuf[lev, 16:24] = c[8:16]
-            cbuf[lev, 24:32] = c[16:24] + s[0:8]
-            cbuf[lev, 32:40] = s[8:16]
+            cbuf[40 * lev + 0 : 40 * lev + 8] = n[0:8]
+            cbuf[40 * lev + 8 : 40 * lev + 16] = n[8:16] + c[0:8]
+            cbuf[40 * lev + 16 : 40 * lev + 24] = c[8:16]
+            cbuf[40 * lev + 24 : 40 * lev + 32] = c[16:24] + s[0:8]
+            cbuf[40 * lev + 32 : 40 * lev + 40] = s[8:16]
+        cw[...] = dot_right(cbuf[...], spread_w[...])
         for e in range(1, ER - 1):
-            even = jnp.broadcast_to(cbuf[0, e : e + 1, :], (8, 128))
-            odd = jnp.broadcast_to(cbuf[1, e : e + 1, :], (8, 128))
-            kc[e] = jnp.where(lev_odd, odd, even) * kbuf[e]
+            for p in range(3):
+                kc[e, p] = by_level(cw, e, 40 + e, p) * kbuf[e, p]
         bufs = (xa, xb)
-        for p in range(2 * NPASS):
-            src, dst = bufs[p % 2], bufs[(p + 1) % 2]
-            row = (lambda r: mf[r] * kc[r][None]) if p == 0 else (lambda r, src=src: src[r])
-
-            def store(r, x, dst=dst, p=p):
-                if p == 2 * NPASS - 1:
-                    acc[r - (HR - 1)] = jnp.sum(x * mf[r], axis=0)
+        for t in range(2 * NPASS):
+            src, dst = bufs[t % 2], bufs[(t + 1) % 2]
+
+            def row(r, src=src, t=t):
+                return [mf[r, p] * kc[r, p][None] if t == 0 else src[r, p] for p in range(3)]
+
+            def store(r, p, x, dst=dst, t=t):
+                if t == 2 * NPASS - 1:
+                    at = 8 * (r - HR + 1)
+                    acc[at : at + 8, 128 * p : 128 * (p + 1)] = jnp.sum(x * mf[r, p], axis=0)
                 else:
-                    dst[r] = x
-
-            middle = p == NPASS - 1
-            diffuse(row, store, rbuf if middle else qbuf, ibuf if middle else kbuf, 2 + p, ER - 2 - p)
-        tall = dot_left(prows_w[...], acc[...].reshape((TR + 2) * 8, 128))
+                    dst[r, p] = x
+
+            middle = t == NPASS - 1
+            diffuse(row, store, rbuf if middle else qbuf, ibuf if middle else kbuf, 2 + t, ER - 2 - t)
+        tall = dot_left(prows_w[...], acc[...])
         scale = sscale[...]
         return scale * scale * v + dot_right(tall, pcols_w[...]) * NINE
 
@@ -331,10 +388,10 @@
 
 def per_device(NX, NY, innovation, obs_weight, static_scale, members, diffusivity):
     wide = members.shape[-1]
-    m = members.reshape(9, 4, 2, 2, wide).transpose(0, 3, 1, 2, 4).reshape(9, 16, wide)
-    k = jnp.broadcast_to(diffusivity.transpose(1, 0, 2)[:, None], (2, 4, 2, wide)).reshape(1, 16, wide)
-    both = jnp.pad(jnp.concatenate([m, k]), ((0, 0), (0, 0), (HC, 128 - TC - HC)))
-    source = jnp.stack([both[:, :, TC * j : TC * j + 128] for j in range(NY)])
+    m = members.reshape(4, 9, 2, 2, wide).transpose(0, 3, 1, 2, 4).reshape(8, 18, wide)
+    m = jnp.pad(m, ((0, 0), (0, 6), (0, 0))).reshape(192, wide)
+    k = jnp.pad(diffusivity.transpose(1, 0, 2).reshape(4, wide), ((0, 12), (0, 0)))
+    raw = jnp.pad(jnp.concatenate([m, k]), ((0, 0), (128, 128)))
     vec = (2 * FR, FC)
     vmem = pl.BlockSpec(memory_space=pltpu.VMEM)
     dma = pltpu.SemaphoreType.DMA
@@ -344,21 +401,28 @@
         in_specs=[vmem] * 4,
         out_specs=(vmem, vmem),
         scratch_shapes=[
-            pltpu.VMEM((PAIRS, 10, 16, 128), BF16),
-            pltpu.VMEM((ER, 9, 8, 128), F32),
-            pltpu.VMEM((ER, 9, 8, 128), F32),
-            pltpu.VMEM((ER, 9, 8, 128), F32),
-            pltpu.VMEM((ER, 8, 128), F32),
-            pltpu.VMEM((ER, 8, 128), F32),
-            pltpu.VMEM((ER, 8, 128), F32),
-            pltpu.VMEM((ER, 8, 128), F32),
-            pltpu.VMEM((ER, 8, 128), F32),
-            pltpu.VMEM((TR + 2, 8, 128), F32),
-            pltpu.VMEM((2, 40, 128), F32),
+            pltpu.VMEM((PAIRS, MSG, 128), BF16),
+            pltpu.VMEM((ER, 3, 3, 8, 128), F32),
+            pltpu.VMEM((ER, 3, 3, 8, 128), F32),
+            pltpu.VMEM((ER, 3, 3, 8, 128), F32),
+            pltpu.VMEM((ER, 3, 8, 128), F32),
+            pltpu.VMEM((ER, 3, 8, 128), F32),
+            pltpu.VMEM((ER, 3, 8, 128), F32),
+            pltpu.VMEM((ER, 3, 8, 128), F32),
+            pltpu.VMEM((ER, 3, 8, 128), F32),
+            pltpu.VMEM(((TR + 2) * 8, 384), F32),
+            pltpu.VMEM((80, 128), F32),
+            pltpu.VMEM((80, 384), F32),
+            pltpu.VMEM((2 * ER, 384), F32),
+            pltpu.VMEM((2 * ER, 128), F32),
+            pltpu.VMEM((NY, MSG + 8, 128), F32),
+            pltpu.VMEM((NY, MSG, 128), BF16),
+            pltpu.VMEM((PAIRS, MSG + 8, 128), F32),
             pltpu.VMEM((112, 2 * FR), F32),
             pltpu.VMEM((FC, 384), BF16),
             pltpu.VMEM((2 * FR, (TR + 2) * 8), BF16),
-            pltpu.VMEM((128, FC), BF16),
+            pltpu.VMEM((384, FC), BF16),
+            pltpu.VMEM((128, 384), BF16),
             pltpu.VMEM((3, 3, 48, 128), F32),
             pltpu.VMEM((3, 3, 32, 128), F32),
             pltpu.VMEM((3, 3, 32, 128), F32),
@@ -379,7 +443,7 @@
         ],
         compiler_params=pltpu.CompilerParams(collective_id=0, has_side_effects=True),
         name="solve",
-    )(innovation.reshape(vec), obs_weight.reshape(vec), static_scale.reshape(vec), source)
+    )(innovation.reshape(vec), obs_weight.reshape(vec), static_scale.reshape(vec), raw)
     return inc.reshape(2, FR, FC), stat.reshape(2, FR, FC)
 
 

time: 74.9 us -> 67.4 us (0.90)
  Pallas kernels: 68.5 us -> 61.7 us
    pallas_call x1, Pallas kernels: 68.5 us -> 61.7 us  [per_device(): pl.pallas_call(functools.partial(kernel, NX, NY), out_shape=(jax.ShapeDty...]
    unnamed x16 -> x7, local copies, waits for them, and re-layouts: 4.26 us -> 2.95 us
    pad x0 -> x2, local copies, waits for them, and re-layouts: none -> 0.76 us  [the longest x1 0.74 us: per_device(): raw = jnp.pad(jnp.concatenate([m, k]), ((0, 0), (128, 128)))]
where the time goes in v3:
time: 67.4 us; the launch traced here: 67.2 us
  Pallas kernels  61.7 us (92%)
  local copies, waits for them, and re-layouts  4.8 us (7%)
  between operations  0.69 us (1%)
    pallas_call x1, Pallas kernels, per_device(): pl.pallas_call(functools.partial(kernel, NX, NY), out_shape=(jax.ShapeDty...  61.7 us
    unnamed x7, local copies, waits for them, and re-layouts  2.95 us

profile of v3, /device:TPU:1, one launch (start us, length us, event | category | flops | bytes accessed | tf_op | source)
XLA Modules:
  0.0 67.2 jit_solution(1972149898907874835)
XLA Ops:
  0.6 0.0 copy-start.1
  0.6 0.7 %copy-done.1 = bf16[2,2,512]{2,1,0:T(2,128)(2,1)S(1)} copy-done((bf16[2,2,512]{2,1,0:T(2,128)(2,1)S(1)}, bf16[2,2,512]{2,1,0:T(2,128)(2,1)}, u32[]{:S(2)}) %copy-start.1) | copy-done | bytes 4120
  1.3 1.0 %copy.14 = bf16[4,9,2,2,512]{4,3,0,2,1:T(2,128)(2,1)S(1)} copy(bf16[4,9,2,2,512]{4,3,2,1,0:T(2,128)(2,1)} %bitcast.15) | data formatting | bytes 294912 | tf_op jit(solution)/shard_map/reshape | solution.py:391
  2.4 0.1 reshape.35
  2.5 0.7 %pad.14.raw = bf16[208,768]{1,0:T(8,128)(2,1)} pad(bf16[208,512]{1,0:T(8,128)(2,1)S(1)} %fusion.1, bf16[]{:T(256)} %constant.2.clone.1), padding=0_0x128_128 | pad | bytes 532482 | tf_op jit(solution)/shard_map/jit(_pad)/pad | solution.py:394
  3.3 61.7 %solve.1 = (f32[96,192]{1,0:T(8,128)}, f32[96,192]{1,0:T(8,128)}) custom-call(f32[96,192]{1,0:T(8,128)} %bitcast.16, f32[96,192]{1,0:T(8,128)} %bitcast.17, f32[96,192]{1,0:T(8,128)} %bitcast.18, bf16[208,768]{1,0:T(8,128)(2,1)} %pad.14.raw), custom_call_target="tpu_custom_call" | custom-call | tf_op jit(solution)/shard_map/solve/pallas_call | solution.py:398
  65.0 0.0 copy-start
  65.0 1.6 %copy.17 = f32[2,48,192]{2,1,0:T(8,128)} copy(f32[2,48,192]{2,1,0:T(8,128)} %bitcast.20) | data formatting | bytes 147456
  66.5 0.0 copy-done
  66.5 0.6 copy.18
  (5 shorter events, 0.1 us)
Async XLA Ops:
  0.6 0.7 %copy-start.1 = (bf16[2,2,512]{2,1,0:T(2,128)(2,1)S(1)}, bf16[2,2,512]{2,1,0:T(2,128)(2,1)}, u32[]{:S(2)}) copy-start(bf16[2,2,512]{2,1,0:T(2,128)(2,1)} %param.9) | copy-start | bytes 12292
  65.0 1.6 %copy-start = (f32[96,192]{1,0:T(8,128)S(1)}, f32[96,192]{1,0:T(8,128)}, u32[]{:S(2)}) copy-start(f32[96,192]{1,0:T(8,128)} %get-tuple-element.5) | copy-start | bytes 221188

commit v4 on v3

--- a/solution.py
+++ b/solution.py
@@ -54,13 +54,14 @@
 
 
 def kernel(
-    NX, NY, innov, wobs, sscale, raw,
+    NX, NY, innov_in, wobs_in, sscale_in, members_in, rates_in,
     inc_ref, stat_ref,
+    innov, wobs, sscale, members, rates, raw,
     mbuf, mf, xa, xb, kbuf, qbuf, ibuf, rbuf, kc, acc, cbuf, cw, kw, kcomp, stage, source, unpacked,
     rows_w, cols_w, prows_w, pcols_w, spread_w,
-    snd_c, snd_n, snd_s, rcv_c, rcv_n, rcv_s,
-    vq, vb, red_own, red_y, red_own2, red_x,
-    m_send, m_recv, m_local, h_send, h_recv, c_send, c_recv, ry_send, ry_recv, rx_send, rx_recv,
+    snd_c, snd_n, snd_s, snd_side, rcv_n, rcv_s, rcv_side,
+    vq, vb, last, red_own, red_y, red_own2, red_x,
+    in_sem, m_send, m_recv, m_local, h_send, h_recv, c_send, c_recv, ry_send, ry_recv, rx_send, rx_recv,
 ):
     gx, gy = lax.axis_index("gx"), lax.axis_index("gy")
     north, south = lax.rem(gx + NX - 1, NX), lax.rem(gx + 1, NX)
@@ -74,6 +75,15 @@
             pl.semaphore_signal(barrier, inc=1, device_id=(row, col), device_id_type=MESH)
     for d in range(1, NY):
         pl.semaphore_signal(barrier, inc=1, device_id=(gx, lax.rem(gy + d, NY)), device_id_type=MESH)
+
+    loads = [
+        pltpu.make_async_copy(src, dst, in_sem.at[i])
+        for i, (src, dst) in enumerate(
+            ((innov_in, innov), (wobs_in, wobs), (sscale_in, sscale), (members_in, members), (rates_in, rates))
+        )
+    ]
+    for copy in loads:
+        copy.start()
 
     has_n = jnp.where(gx > 0, 1, 0)
     has_s = jnp.where(gx < NX - 1, 1, 0)
@@ -91,30 +101,34 @@
             fine = iota(shape, 1) - FR * lev
             value = jnp.where((fine >= 0) & (fine < FR), weight(fine, iota(shape, 0) + shift) * on, 0)
             rows_w[start + count * lev : start + count * (lev + 1), :] = value.astype(F32)
-    shape = (2 * FR, (TR + 2) * 8)
-    lev_of = jnp.where(iota(shape, 0) >= FR, 1, 0)
-    inner = iota(shape, 1)
-    value = jnp.where((inner & 1) == lev_of, weight(iota(shape, 0) - FR * lev_of, (inner >> 3) - 1), 0)
-    prows_w[...] = value.astype(F32).astype(BF16)
-    for p in range(3):
-        shape = (128, FC)
-        at = iota(shape, 0) & 31
-        value = jnp.where(at < POS, weight(iota(shape, 1), 3 * at + p - HC), 0)
-        pcols_w[128 * p : 128 * (p + 1)] = value.astype(F32).astype(BF16)
-        shape = (128, 128)
-        at = iota(shape, 1) & 31
-        value = jnp.where((at < POS) & (iota(shape, 0) == 32 * p + at), 1, 0)
-        spread_w[:, 128 * p : 128 * (p + 1)] = value.astype(F32).astype(BF16)
+    place = iota((8, 128), 1) & 31
+
+    def squeeze(x, side):
+        out = jnp.zeros((8, 128), F32)
+        for i in range(x.shape[0] // 8):
+            turn = (4 * i - (0 if side == 2 else POS - 4)) % 128
+            block = x[8 * i : 8 * i + 8]
+            out = jnp.where((place >> 2) == i, pltpu.roll(block, turn, 1) if turn else block, out)
+        return out
+
+    def spread_out(x, count, side):
+        base = 0 if side == 2 else POS - 4
+        out = []
+        for i in range(count):
+            turn = (base - 4 * i) % 128
+            out.append(jnp.where((place >> 2) == base // 4, pltpu.roll(x, turn, 1) if turn else x, 0.0))
+        return jnp.concatenate(out)
 
     def c_copies(app):
         found = []
-        for b, col in ((0, west), (1, gy), (2, east)):
-            for kind, (row, snd, rcv) in enumerate(((gx, snd_c, rcv_c), (north, snd_n, rcv_n), (south, snd_s, rcv_s))):
+        for b, col in ((0, west), (2, east), (1, gy)):
+            for kind, (row, snd, rcv) in enumerate(((gx, snd_c, snd_c), (north, snd_n, rcv_n), (south, snd_s, rcv_s))):
                 if b == 1 and kind == 0:
                     continue
                 found.append(
                     pltpu.make_async_remote_copy(
-                        src_ref=snd.at[app, b], dst_ref=rcv.at[app, b],
+                        src_ref=snd.at[app] if b == 1 else snd_side.at[app, kind, b // 2],
+                        dst_ref=rcv.at[app] if b == 1 else rcv_side.at[app, kind, b // 2],
                         send_sem=c_send.at[app, kind, b], recv_sem=c_recv.at[app, kind, b],
                         device_id=(row, col), device_id_type=MESH,
                     )
@@ -124,15 +138,41 @@
     def restrict(app, v):
         wide = dot_right(v, cols_w[...])
         z = dot_left(rows_w[...].astype(BF16), wide) * NINE
-        for b in range(3):
-            snd_c[app, b] = z[0:48, 128 * b : 128 * (b + 1)]
-            snd_n[app, b] = z[48:80, 128 * b : 128 * (b + 1)]
-            snd_s[app, b] = z[80:112, 128 * b : 128 * (b + 1)]
-
+        for kind, (start, count, ref) in enumerate(((0, 48, snd_c), (48, 32, snd_n), (80, 32, snd_s))):
+            for b in (0, 2):
+                snd_side[app, kind, b // 2] = squeeze(z[start : start + count, 128 * b : 128 * (b + 1)], b)
+            ref[app] = z[start : start + count, 128:256]
+
+    loads[0].wait()
+    loads[1].wait()
     first = wobs[...] * innov[...]
     vq[0] = first
     restrict(0, first)
 
+    loads[3].wait()
+    loads[4].wait()
+    wide = members.shape[-1]
+    natural = members[...].astype(F32).reshape(144, wide).astype(BF16)
+    shape = (24, 144)
+    at = iota(shape, 0)
+    zero = jnp.zeros((208, 128), BF16)
+    raw[:, 0:128] = zero
+    raw[:, 128 + wide : 256 + wide] = zero
+    order = []
+    for g in range(4):
+        for row in range(2):
+            value = jnp.where((at < 18) & (iota(shape, 1) == (9 * g + (at >> 1)) * 4 + (at & 1) * 2 + row), 1, 0)
+            order.append(value.astype(F32).astype(BF16))
+    raw[0:192, 128 : 128 + wide] = jnp.dot(
+        jnp.concatenate(order), natural, preferred_element_type=F32
+    ).astype(BF16)
+    by_lev = rates[...].astype(F32).reshape(4, wide)
+    kcomp[0:16] = jnp.zeros((16, 128), F32)
+    for tile in range(wide // 128):
+        lanes = slice(128 * tile, 128 * (tile + 1))
+        for at_row, of in enumerate((0, 2, 1, 3)):
+            kcomp[at_row : at_row + 1] = by_lev[of : of + 1, lanes]
+        raw[192:208, 128 + 128 * tile : 256 + 128 * tile] = kcomp[0:16].astype(BF16)
     group = iota((24, 128), 1) >> 5
     for odd in range(2):
         shape = (256, 128)
@@ -175,6 +215,21 @@
     own = pltpu.make_async_copy(source.at[gy], mbuf.at[gy + 5], m_local)
     own.start()
 
+    shape = (2 * FR, (TR + 2) * 8)
+    lev_of = jnp.where(iota(shape, 0) >= FR, 1, 0)
+    inner = iota(shape, 1)
+    value = jnp.where((inner & 1) == lev_of, weight(iota(shape, 0) - FR * lev_of, (inner >> 3) - 1), 0)
+    prows_w[...] = value.astype(F32).astype(BF16)
+    for p in range(3):
+        shape = (128, FC)
+        at = iota(shape, 0) & 31
+        value = jnp.where(at < POS, weight(iota(shape, 1), 3 * at + p - HC), 0)
+        pcols_w[128 * p : 128 * (p + 1)] = value.astype(F32).astype(BF16)
+        shape = (128, 128)
+        at = iota(shape, 1) & 31
+        value = jnp.where((at < POS) & (iota(shape, 0) == 32 * p + at), 1, 0)
+        spread_w[:, 128 * p : 128 * (p + 1)] = value.astype(F32).astype(BF16)
+
     def halo(side, d):
         g = lax.rem(gy + NY - d, NY)
         return g <= 4 if side == 0 else g >= 3, pltpu.make_async_remote_copy(
@@ -208,6 +263,7 @@
                 mf[2 * pair + row, p] = x.reshape(3, 8, 128)
         kcomp[4 * pair : 4 * pair + 4] = unpacked[pair, MSG - 4 : MSG]
 
+    loads[2].wait()
     for pair in range(5, 13):
         unpack(pair)
     for d in range(NY):
@@ -238,9 +294,14 @@
     def apply(app, v):
         for copy in c_copies(app):
             copy.wait_recv()
-        mine = snd_c[app, 1] + rcv_c[app, 0] + rcv_c[app, 2]
-        north_in = rcv_s[app, 0] + rcv_s[app, 1] + rcv_s[app, 2]
-        south_in = rcv_n[app, 0] + rcv_n[app, 1] + rcv_n[app, 2]
+        def total(kind, middle):
+            count = middle.shape[0] // 8
+            sides = [spread_out(rcv_side[app, kind, b // 2], count, b) for b in (0, 2)]
+            return middle + (sides[0] + sides[1])
+
+        mine = total(0, snd_c[app])
+        north_in = total(2, rcv_s[app])
+        south_in = total(1, rcv_n[app])
         for lev in range(2):
             c, n, s = mine[24 * lev : 24 * lev + 24], north_in[16 * lev : 16 * lev + 16], south_in[16 * lev : 16 * lev + 16]
             cbuf[40 * lev + 0 : 40 * lev + 8] = n[0:8]
@@ -274,11 +335,11 @@
 
     lane = iota((1, 128), 1)
 
-    def pack(pairs):
+    def pack(pairs, first=0):
         out = jnp.zeros((1, 128), F32)
         for i, (left, right) in enumerate(pairs):
             total = jnp.sum(jnp.sum(left * right, axis=0, keepdims=True), axis=1, keepdims=True)
-            out = jnp.where(lane == i, total, out)
+            out = jnp.where(lane == i + first, total, out)
         return out
 
     def y_copy(use, d):
@@ -335,30 +396,33 @@
     vq[1] = q1
     reduce_middle(0)
     b1 = apply(1, vq[1])
-    sums = reduce_end(0)
-    theta = pick(sums, 1) / pick(sums, 0)
-    b1 = b1 - theta * vb[0]
-    vq[1] = vq[1] - theta * vq[0]
-    vb[1] = b1
     q2 = w * b1
     restrict(2, q2)
     for copy in c_copies(2):
         copy.start()
     vq[2] = q2
-    b2 = apply(2, vq[2])
+    sums = reduce_end(0)
+    theta = pick(sums, 1) / pick(sums, 0)
+    last[1] = theta * b1
+    q0, b0 = vq[0], vb[0]
+    q2 = q2 - theta * vq[1]
+    last[0] = q2
+    q1 = vq[1] - theta * q0
+    vq[1] = q1
+    b1 = b1 - theta * b0
+    vb[1] = b1
+    early = pack(((q0, b0), (q0, b1), (b0, q2), (q1, b1), (b1, q2), (b0, w * b0), (b0, w * b1), (b1, w * b1)))
+    b2 = apply(2, vq[2]) - last[1]
     vb[2] = b2
-    q0, q1, b0, b1 = vq[0], vq[1], vb[0], vb[1]
-    wb = (w * b0, w * b1, w * b2)
-    q2 = vq[2]
-    row = pack((
-        (q0, b0), (q0, b1), (q0, b2), (q1, b1), (q1, b2), (q2, b2),
-        (b0, wb[0]), (b0, wb[1]), (b0, wb[2]), (b1, wb[1]), (b1, wb[2]), (b2, wb[2]),
-    ))
+    vq[2] = last[0]
+    late = pack(((vq[2], b2), (b2, wobs[...] * b2)), 8)
+    row = jnp.where(lane >= 8, late, early)
     reduce_start(1, row)
     reduce_middle(1)
     sums = reduce_end(1)
-    e = [pick(sums, i) for i in range(12)]
-    s00, s01, s02, s11, s12, s22 = [e[i] + e[6 + i] for i in range(6)]
+    e00, e01, e02, e11, e12, f00, f01, f11, e22, f22 = [pick(sums, i) for i in range(10)]
+    s00, s01, s02 = e00 + f00, e01 + f01, e02 + (e12 + theta * e02)
+    s11, s12, s22 = e11 + f11, e12 + e22, e22 + f22
     tiny = 1e-7
     i0 = 1.0 / s00
     l10, l20 = s01 * i0, s02 * i0
@@ -368,7 +432,7 @@
     l21 = t12 * i1
     d2 = s22 - l20 * s02 - l21 * t12
     i2 = jnp.where(d2 > tiny * s22, 1.0 / d2, 0.0)
-    r0, r1, r2 = e[0], e[1], e[2]
+    r0, r1, r2 = e00, e01, e02
     r1 = r1 - l10 * r0
     r2 = r2 - l20 * r0 - l21 * r1
     z2 = r2 * i2
@@ -387,20 +451,21 @@
 
 
 def per_device(NX, NY, innovation, obs_weight, static_scale, members, diffusivity):
-    wide = members.shape[-1]
-    m = members.reshape(4, 9, 2, 2, wide).transpose(0, 3, 1, 2, 4).reshape(8, 18, wide)
-    m = jnp.pad(m, ((0, 0), (0, 6), (0, 0))).reshape(192, wide)
-    k = jnp.pad(diffusivity.transpose(1, 0, 2).reshape(4, wide), ((0, 12), (0, 0)))
-    raw = jnp.pad(jnp.concatenate([m, k]), ((0, 0), (128, 128)))
     vec = (2 * FR, FC)
     vmem = pl.BlockSpec(memory_space=pltpu.VMEM)
     dma = pltpu.SemaphoreType.DMA
     inc, stat = pl.pallas_call(
         functools.partial(kernel, NX, NY),
         out_shape=(jax.ShapeDtypeStruct(vec, F32), jax.ShapeDtypeStruct(vec, F32)),
-        in_specs=[vmem] * 4,
+        in_specs=[pl.BlockSpec(memory_space=pl.ANY)] * 5,
         out_specs=(vmem, vmem),
         scratch_shapes=[
+            pltpu.VMEM(vec, F32),
+            pltpu.VMEM(vec, F32),
+            pltpu.VMEM(vec, F32),
+            pltpu.VMEM(members.shape, BF16),
+            pltpu.VMEM(diffusivity.shape, BF16),
+            pltpu.VMEM((208, members.shape[-1] + 256), BF16),
             pltpu.VMEM((PAIRS, MSG, 128), BF16),
             pltpu.VMEM((ER, 3, 3, 8, 128), F32),
             pltpu.VMEM((ER, 3, 3, 8, 128), F32),
@@ -423,19 +488,21 @@
             pltpu.VMEM((2 * FR, (TR + 2) * 8), BF16),
             pltpu.VMEM((384, FC), BF16),
             pltpu.VMEM((128, 384), BF16),
-            pltpu.VMEM((3, 3, 48, 128), F32),
-            pltpu.VMEM((3, 3, 32, 128), F32),
-            pltpu.VMEM((3, 3, 32, 128), F32),
-            pltpu.VMEM((3, 3, 48, 128), F32),
-            pltpu.VMEM((3, 3, 32, 128), F32),
-            pltpu.VMEM((3, 3, 32, 128), F32),
+            pltpu.VMEM((3, 48, 128), F32),
+            pltpu.VMEM((3, 32, 128), F32),
+            pltpu.VMEM((3, 32, 128), F32),
+            pltpu.VMEM((3, 3, 2, 8, 128), F32),
+            pltpu.VMEM((3, 32, 128), F32),
+            pltpu.VMEM((3, 32, 128), F32),
+            pltpu.VMEM((3, 3, 2, 8, 128), F32),
             pltpu.VMEM((3,) + vec, F32),
             pltpu.VMEM((3,) + vec, F32),
+            pltpu.VMEM((2,) + vec, F32),
             pltpu.VMEM((2, 1, 128), F32),
             pltpu.VMEM((2, NY, 1, 128), F32),
             pltpu.VMEM((2, 1, 128), F32),
             pltpu.VMEM((2, NX, 1, 128), F32),
-            dma((NY,)), dma((NY,)), dma,
+            dma((5,)), dma((NY,)), dma((NY,)), dma,
             dma((2, NY)), dma((2, NY)),
             dma((3, 3, 3)), dma((3, 3, 3)),
             dma((2, NY)), dma((2, NY)),
@@ -443,7 +510,7 @@
         ],
         compiler_params=pltpu.CompilerParams(collective_id=0, has_side_effects=True),
         name="solve",
-    )(innovation.reshape(vec), obs_weight.reshape(vec), static_scale.reshape(vec), raw)
+    )(innovation.reshape(vec), obs_weight.reshape(vec), static_scale.reshape(vec), members, diffusivity)
     return inc.reshape(2, FR, FC), stat.reshape(2, FR, FC)
 
 

time: 67.4 us -> 58.7 us (0.87)
  Pallas kernels: 61.7 us -> 55.7 us
  local copies, waits for them, and re-layouts: 4.8 us -> 2.22 us
    pallas_call x1, Pallas kernels: 61.7 us -> 55.7 us  [per_device(): pl.pallas_call(functools.partial(kernel, NX, NY), out_shape=(jax.ShapeDty...]
    reshape x3 -> x0, local copies, waits for them, and re-layouts: 1.1 us -> none  [the longest x2 1.08 us: per_device(): members.reshape(4, 9, 2, 2, wide).transpose(0, 3, 1, 2, 4)]
    pad x2 -> x0, local copies, waits for them, and re-layouts: 0.76 us -> none  [the longest x1 0.74 us: per_device(): raw = jnp.pad(jnp.concatenate([m, k]), ((0, 0), (128, 128)))]
    unnamed x7 -> x4, local copies, waits for them, and re-layouts: 2.95 us -> 2.22 us
where the time goes in v4:
time: 58.7 us; the launch traced here: 58.6 us
  Pallas kernels  55.7 us (95%)
  local copies, waits for them, and re-layouts  2.22 us (4%)
  between operations  0.65 us (1%)
    pallas_call x1, Pallas kernels, per_device(): pl.pallas_call(functools.partial(kernel, NX, NY), out_shape=(jax.ShapeDty...  55.7 us
    unnamed x4, local copies, waits for them, and re-layouts  2.22 us

profile of v4, /device:TPU:1, one launch (start us, length us, event | category | flops | bytes accessed | tf_op | source)
XLA Modules:
  0.0 58.6 jit_solution(10344156957748285163)
XLA Ops:
  0.6 55.7 %solve.1 = (f32[96,192]{1,0:T(8,128)}, f32[96,192]{1,0:T(8,128)}) custom-call(f32[96,192]{1,0:T(8,128)} %bitcast.5, f32[96,192]{1,0:T(8,128)} %bitcast.6, f32[96,192]{1,0:T(8,128)} %bitcast.7, bf16[36,2,2,512]{3,2,1,0:T(2,128)(2,1)} %members_in.1, bf16[2,2,512]{2,1,0:T(2,128)(2,1)} %rates_in.1), custom_call_target="tpu_custom_call" | custom-call | tf_op jit(solution)/shard_map/solve/pallas_call | solution.py:457
  56.4 0.0 copy-start
  56.4 1.6 %copy.9 = f32[2,48,192]{2,1,0:T(8,128)} copy(f32[2,48,192]{2,1,0:T(8,128)} %bitcast.9) | data formatting | bytes 147456
  58.0 0.0 copy-done
  58.0 0.6 %copy.10 = f32[2,48,192]{2,1,0:T(8,128)} copy(f32[2,48,192]{2,1,0:T(8,128)S(1)} %bitcast.8) | data formatting | bytes 147456
Async XLA Ops:
  56.4 1.6 %copy-start = (f32[96,192]{1,0:T(8,128)S(1)}, f32[96,192]{1,0:T(8,128)}, u32[]{:S(2)}) copy-start(f32[96,192]{1,0:T(8,128)} %get-tuple-element.5) | copy-start | bytes 221188

commit v5 on v4

--- a/solution.py
+++ b/solution.py
@@ -27,10 +27,7 @@
 
 def parts(x):
     high = x.astype(BF16)
-    rest = x - high.astype(F32)
-    mid = rest.astype(BF16)
-    low = (rest - mid.astype(F32)).astype(BF16)
-    return high, mid, low
+    return high, (x - high.astype(F32)).astype(BF16)
 
 
 def dot_left(const, x):
@@ -68,10 +65,21 @@
     west, east = lax.rem(gy + NY - 1, NY), lax.rem(gy + 1, NY)
 
     barrier = pltpu.get_barrier_semaphore()
-    for d in sorted(range(1, NX), key=lambda d: min(d % 8, 8 - d % 8), reverse=True):
-        pl.semaphore_signal(barrier, inc=1, device_id=(lax.rem(gx + d, NX), gy), device_id_type=MESH)
+
+    def along_z(d):
+        z = lax.rem(2 * lax.div(gx, 8) + lax.rem(gy, 2) + d, NX // 4)
+        return 8 * lax.div(z, 2) + lax.rem(gx, 8), 2 * lax.div(gy, 2) + lax.rem(z, 2)
+
+    def in_plane(d):
+        u = lax.rem(4 * lax.rem(gx, 8) + lax.div(gy, 2) + d, 4 * NY)
+        return 8 * lax.div(gx, 8) + lax.div(u, 4), 2 * lax.rem(u, 4) + lax.rem(gy, 2)
+
+    for d in range(1, NX // 4):
+        pl.semaphore_signal(barrier, inc=1, device_id=along_z(d), device_id_type=MESH)
+    for d in range(1, 4 * NY):
+        pl.semaphore_signal(barrier, inc=1, device_id=in_plane(d), device_id_type=MESH)
     for row in (north, south):
-        for col in (west, east):
+        for col in (west, gy, east):
             pl.semaphore_signal(barrier, inc=1, device_id=(row, col), device_id_type=MESH)
     for d in range(1, NY):
         pl.semaphore_signal(barrier, inc=1, device_id=(gx, lax.rem(gy + d, NY)), device_id_type=MESH)
@@ -85,22 +93,6 @@
     for copy in loads:
         copy.start()
 
-    has_n = jnp.where(gx > 0, 1, 0)
-    has_s = jnp.where(gx < NX - 1, 1, 0)
-    has_w = jnp.where(gy > 0, 1, 0)
-    has_e = jnp.where(gy < NY - 1, 1, 0)
-    for b, on in ((0, has_w), (1, 1), (2, has_e)):
-        shape = (FC, 128)
-        at = iota(shape, 1)
-        cell = 3 * (at & 31) + (at >> 5) - HC + TC * (b - 1)
-        value = jnp.where(((at & 31) < POS) & (at < 96), weight(iota(shape, 0), cell) * on, 0)
-        cols_w[:, 128 * b : 128 * (b + 1)] = value.astype(F32).astype(BF16)
-    for start, count, shift, on in ((0, 24, -2, 1), (48, 16, -2, has_n), (80, 16, 6, has_s)):
-        shape = (count, 2 * FR)
-        for lev in range(2):
-            fine = iota(shape, 1) - FR * lev
-            value = jnp.where((fine >= 0) & (fine < FR), weight(fine, iota(shape, 0) + shift) * on, 0)
-            rows_w[start + count * lev : start + count * (lev + 1), :] = value.astype(F32)
     place = iota((8, 128), 1) & 31
 
     def squeeze(x, side):
@@ -142,12 +134,6 @@
             for b in (0, 2):
                 snd_side[app, kind, b // 2] = squeeze(z[start : start + count, 128 * b : 128 * (b + 1)], b)
             ref[app] = z[start : start + count, 128:256]
-
-    loads[0].wait()
-    loads[1].wait()
-    first = wobs[...] * innov[...]
-    vq[0] = first
-    restrict(0, first)
 
     loads[3].wait()
     loads[4].wait()
@@ -195,10 +181,7 @@
             stage[j, MSG - 4 : MSG] = cut[192:196]
             source[j] = stage[j, 0:MSG].astype(BF16)
 
-    pl.semaphore_wait(barrier, (NY - 1) + (NX - 1) + 4)
-
-    for copy in c_copies(0):
-        copy.start()
+    pl.semaphore_wait(barrier, (NX // 4 - 1) + (4 * NY - 1) + 6 + (NY - 1))
 
     moves = []
     for d in range(1, NY):
@@ -214,6 +197,30 @@
         copy.start()
     own = pltpu.make_async_copy(source.at[gy], mbuf.at[gy + 5], m_local)
     own.start()
+
+    has_n = jnp.where(gx > 0, 1, 0)
+    has_s = jnp.where(gx < NX - 1, 1, 0)
+    has_w = jnp.where(gy > 0, 1, 0)
+    has_e = jnp.where(gy < NY - 1, 1, 0)
+    for b, on in ((0, has_w), (1, 1), (2, has_e)):
+        shape = (FC, 128)
+        at = iota(shape, 1)
+        cell = 3 * (at & 31) + (at >> 5) - HC + TC * (b - 1)
+        value = jnp.where(((at & 31) < POS) & (at < 96), weight(iota(shape, 0), cell) * on, 0)
+        cols_w[:, 128 * b : 128 * (b + 1)] = value.astype(F32).astype(BF16)
+    for start, count, shift, on in ((0, 24, -2, 1), (48, 16, -2, has_n), (80, 16, 6, has_s)):
+        shape = (count, 2 * FR)
+        for lev in range(2):
+            fine = iota(shape, 1) - FR * lev
+            value = jnp.where((fine >= 0) & (fine < FR), weight(fine, iota(shape, 0) + shift) * on, 0)
+            rows_w[start + count * lev : start + count * (lev + 1), :] = value.astype(F32)
+    loads[0].wait()
+    loads[1].wait()
+    first = wobs[...] * innov[...]
+    vq[0] = first
+    restrict(0, first)
+    for copy in c_copies(0):
+        copy.start()
 
     shape = (2 * FR, (TR + 2) * 8)
     lev_of = jnp.where(iota(shape, 0) >= FR, 1, 0)
@@ -345,13 +352,13 @@
     def y_copy(use, d):
         return pltpu.make_async_remote_copy(
             src_ref=red_own.at[use], dst_ref=red_y.at[use, d], send_sem=ry_send.at[use, d], recv_sem=ry_recv.at[use, d],
-            device_id=(gx, lax.rem(gy + d, NY)), device_id_type=MESH,
+            device_id=along_z(d), device_id_type=MESH,
         )
 
     def x_copy(use, d):
         return pltpu.make_async_remote_copy(
             src_ref=red_own2.at[use], dst_ref=red_x.at[use, d], send_sem=rx_send.at[use, d], recv_sem=rx_recv.at[use, d],
-            device_id=(lax.rem(gx + d, NX), gy), device_id_type=MESH,
+            device_id=in_plane(d), device_id_type=MESH,
         )
 
     def each(count, make, what):

time: 58.7 us -> 56.7 us (0.966)
  Pallas kernels: 55.7 us -> 53.7 us
    pallas_call x1, Pallas kernels: 55.7 us -> 53.7 us  [per_device(): pl.pallas_call(functools.partial(kernel, NX, NY), out_shape=(jax.ShapeDty...]
where the time goes in v5:
time: 56.7 us; the launch traced here: 56.6 us
  Pallas kernels  53.7 us (95%)
  local copies, waits for them, and re-layouts  2.22 us (4%)
  between operations  0.65 us (1%)
    pallas_call x1, Pallas kernels, per_device(): pl.pallas_call(functools.partial(kernel, NX, NY), out_shape=(jax.ShapeDty...  53.7 us
    unnamed x4, local copies, waits for them, and re-layouts  2.22 us

profile of v5, /device:TPU:1, one launch (start us, length us, event | category | flops | bytes accessed | tf_op | source)
XLA Modules:
  0.0 56.6 jit_solution(17663817615112541030)
XLA Ops:
  0.6 53.7 %solve.1 = (f32[96,192]{1,0:T(8,128)}, f32[96,192]{1,0:T(8,128)}) custom-call(f32[96,192]{1,0:T(8,128)} %bitcast.5, f32[96,192]{1,0:T(8,128)} %bitcast.6, f32[96,192]{1,0:T(8,128)} %bitcast.7, bf16[36,2,2,512]{3,2,1,0:T(2,128)(2,1)} %members_in.1, bf16[2,2,512]{2,1,0:T(2,128)(2,1)} %rates_in.1), custom_call_target="tpu_custom_call" | custom-call | tf_op jit(solution)/shard_map/solve/pallas_call | solution.py:464
  54.3 0.0 copy-start
  54.4 1.6 %copy.9 = f32[2,48,192]{2,1,0:T(8,128)} copy(f32[2,48,192]{2,1,0:T(8,128)} %bitcast.9) | data formatting | bytes 147456
  55.9 0.0 copy-done
  55.9 0.6 %copy.10 = f32[2,48,192]{2,1,0:T(8,128)} copy(f32[2,48,192]{2,1,0:T(8,128)S(1)} %bitcast.8) | data formatting | bytes 147456
Async XLA Ops:
  54.3 1.6 %copy-start = (f32[96,192]{1,0:T(8,128)S(1)}, f32[96,192]{1,0:T(8,128)}, u32[]{:S(2)}) copy-start(f32[96,192]{1,0:T(8,128)} %get-tuple-element.5) | copy-start | bytes 221188

commit v6 on v5

--- a/solution.py
+++ b/solution.py
@@ -74,13 +74,13 @@
         u = lax.rem(4 * lax.rem(gx, 8) + lax.div(gy, 2) + d, 4 * NY)
         return 8 * lax.div(gx, 8) + lax.div(u, 4), 2 * lax.rem(u, 4) + lax.rem(gy, 2)
 
-    for d in range(1, NX // 4):
+    for row in (north, south):
+        for col in (west, east, gy):
+            pl.semaphore_signal(barrier, inc=1, device_id=(row, col), device_id_type=MESH)
+    for d in (4, 3, 5, 2, 6, 1, 7):
         pl.semaphore_signal(barrier, inc=1, device_id=along_z(d), device_id_type=MESH)
     for d in range(1, 4 * NY):
         pl.semaphore_signal(barrier, inc=1, device_id=in_plane(d), device_id_type=MESH)
-    for row in (north, south):
-        for col in (west, gy, east):
-            pl.semaphore_signal(barrier, inc=1, device_id=(row, col), device_id_type=MESH)
     for d in range(1, NY):
         pl.semaphore_signal(barrier, inc=1, device_id=(gx, lax.rem(gy + d, NY)), device_id_type=MESH)
 

time: 56.7 us -> 56.2 us (level)
  no operation moved by 1% of the time
where the time goes in v6:
time: 56.2 us; the launch traced here: 56 us
  Pallas kernels  53.2 us (95%)
  local copies, waits for them, and re-layouts  2.22 us (4%)
  between operations  0.65 us (1%)
    pallas_call x1, Pallas kernels, per_device(): pl.pallas_call(functools.partial(kernel, NX, NY), out_shape=(jax.ShapeDty...  53.2 us
    unnamed x4, local copies, waits for them, and re-layouts  2.22 us

profile of v6, /device:TPU:1, one launch (start us, length us, event | category | flops | bytes accessed | tf_op | source)
XLA Modules:
  0.0 56.0 jit_solution(7106536765448953127)
XLA Ops:
  0.6 53.2 %solve.1 = (f32[96,192]{1,0:T(8,128)}, f32[96,192]{1,0:T(8,128)}) custom-call(f32[96,192]{1,0:T(8,128)} %bitcast.5, f32[96,192]{1,0:T(8,128)} %bitcast.6, f32[96,192]{1,0:T(8,128)} %bitcast.7, bf16[36,2,2,512]{3,2,1,0:T(2,128)(2,1)} %members_in.1, bf16[2,2,512]{2,1,0:T(2,128)(2,1)} %rates_in.1), custom_call_target="tpu_custom_call" | custom-call | tf_op jit(solution)/shard_map/solve/pallas_call | solution.py:464
  53.8 0.0 copy-start
  53.8 1.6 %copy.9 = f32[2,48,192]{2,1,0:T(8,128)} copy(f32[2,48,192]{2,1,0:T(8,128)} %bitcast.9) | data formatting | bytes 147456
  55.4 0.0 copy-done
  55.4 0.6 %copy.10 = f32[2,48,192]{2,1,0:T(8,128)} copy(f32[2,48,192]{2,1,0:T(8,128)S(1)} %bitcast.8) | data formatting | bytes 147456
Async XLA Ops:
  53.8 1.6 %copy-start = (f32[96,192]{1,0:T(8,128)S(1)}, f32[96,192]{1,0:T(8,128)}, u32[]{:S(2)}) copy-start(f32[96,192]{1,0:T(8,128)} %get-tuple-element.5) | copy-start | bytes 221188
